TPU v7x, 32 devices: a whole 2x2x4 slice. The times are simulated.
32 devices in a mesh: row: 4 (over y, x), col: 8 (over z, core).
Axes of the slice: x: 2, y: 2, z: 4, core: 2. Of those that a mesh axis runs over, the one named last changes fastest.
Arguments:
- left_tiles: bfloat16 [2, 32, 256, 256], P(None, 'row', 'col'), may hold values from 0.02 to 3, as said below
- right_tile_store: bfloat16 [32, 24, 256, 256], P('col', 'row'), may hold values from 0.019897461 to 1
- right_index: int32 [32, 24], P('col', 'row'), may hold values from 0 to 7, as said below
- right_count: int32 [32, 4], P('col', 'row'), may hold values from 1 to 6
Outputs:
- inflated: bfloat16 [2, 32, 256, 256], P(None, 'col', 'row')
Inputs may be any that keep to these rules, and one draw needn't show every extreme that they name: `right_index`: for each column block and each row index the 6 slots name distinct contraction blocks; only the first right_count of them are used. `left_tiles`: positive entries.
All inputs are finite; a program needn't handle non-finite values.
Results may differ from a plain program's by a relative error of at most 0.001.
Values may be sent and summed in bfloat16 or wider, within the bound.
No kernel may reach another device: no remote copies, remote signals or barrier semaphores. Data moves between devices by JAX's collectives and lax.ppermute only.
A program may use at most 64 MiB of HBM per device.

v0:
```python
import functools
import jax
import jax.numpy as jnp
from jax import lax
from jax.experimental import pallas as pl
from jax.experimental.pallas import tpu as pltpu
from jax.sharding import PartitionSpec as P


LEVELS = 65280.0
OFFSET = 32640
LOG_STEPS = 256.0
CODE_ROWS = 16
MAX_DIRECT = 8

VMEM = pl.BlockSpec(memory_space=pltpu.VMEM)
SMEM = pl.BlockSpec(memory_space=pltpu.SMEM)


def stage_kernel(right_ref, out_ref, sems):
    copies = [
        pltpu.make_async_copy(right_ref.at[j], out_ref.at[j], sems.at[j])
        for j in range(right_ref.shape[0])
    ]
    for copy in copies:
        copy.start()
    for copy in copies:
        copy.wait()


def product_kernel(n_row, shifts, index_ref, count_ref, *refs):
    n_block = len(shifts)
    blocks, right_ref = refs[:n_block], refs[n_block]
    own_ref = refs[n_block + 1]
    sent_refs = refs[n_block + 2 : n_block + 1 + n_row]
    left, partial = refs[-2:]
    column_blocks, slots, tile, _ = right_ref.shape
    kept = left.shape[0] - 1
    part = tile // n_row
    row = lax.axis_index("row")
    for block, shift in zip(blocks, shifts):
        rows = block.shape[1]
        if n_block == 1:
            left[:kept] = block[...]
        else:
            start = pl.multiple_of((lax.axis_index("col") ^ shift) * rows, rows)
            left[:kept, pl.ds(start, rows), :] = block[...]
    left[kept] = jnp.zeros(left.shape[1:], left.dtype)
    lines = lax.broadcasted_iota(jnp.int32, (CODE_ROWS, tile), 0)
    codes = jnp.zeros((CODE_ROWS, tile), jnp.int32)
    for j in range(column_blocks):
        total = None
        for q in range(slots):
            picked = jnp.where(q < count_ref[j], index_ref[j, q], kept)
            term = jnp.dot(left[picked], right_ref[j, q], preferred_element_type=jnp.float32)
            total = term if total is None else total + term
        partial[...] = total
        top = jnp.max(total, axis=0, keepdims=True)
        code = jnp.floor(jnp.log2(top) * LOG_STEPS).astype(jnp.int32) + 2
        grow = LEVELS * jnp.exp2(code.astype(jnp.float32) * (-1.0 / LOG_STEPS))
        codes = jnp.where(lines == j, code, codes)
        own_ref[j] = partial[pl.ds(pl.multiple_of(row * part, part), part), :]
        for k in range(1, n_row):
            peer = row ^ k
            value = partial[pl.ds(pl.multiple_of(peer * part, part), part), :]
            coded = (value * grow + 0.5).astype(jnp.int32) - OFFSET
            sent_refs[k - 1][j * part : (j + 1) * part, :] = coded.astype(jnp.int16)
    for sent in sent_refs:
        sent[column_blocks * part :, :] = codes.astype(jnp.int16)


def reduce_kernel(n_row, has_before, *refs):
    got_refs = refs[: n_row - 1]
    own_ref = refs[n_row - 1]
    before_ref = refs[n_row] if has_before else None
    squared_ref, sums_ref = refs[-2:]
    column_blocks, part, _ = own_ref.shape
    shrinks = []
    for got in got_refs:
        code = got[column_blocks * part :, :].astype(jnp.int32)
        shrinks.append(jnp.exp2(code.astype(jnp.float32) * (1.0 / LOG_STEPS)) * (1.0 / LEVELS))
    for j in range(column_blocks):
        total = own_ref[j]
        for got, shrink in zip(got_refs, shrinks):
            coded = got[j * part : (j + 1) * part, :].astype(jnp.int32) + OFFSET
            total = total + coded.astype(jnp.float32) * shrink[j : j + 1]
        squared = total * total
        squared_ref[j] = squared
        sums = jnp.sum(squared, axis=0, keepdims=True)
        if has_before:
            sums = sums + before_ref[j : j + 1]
        sums_ref[j : j + 1] = sums


def scale_kernel(windows, n_row, *refs):
    squared_refs = refs[:windows]
    sums_refs = refs[windows : windows + n_row]
    out_ref = refs[-1]
    column_blocks = out_ref.shape[1]
    tile = out_ref.shape[3]
    total = sums_refs[0][...]
    for other in sums_refs[1:]:
        total = total + other[...]
    scale = (windows * tile) / total
    for a in range(windows):
        for j in range(column_blocks):
            out_ref[a, j] = (squared_refs[a][j] * scale[j : j + 1]).astype(out_ref.dtype)


def exchange(x, axis, n, k, flip=False):
    pairs = [(i, i ^ k) for i in range(n)]
    return lax.ppermute(x, axis, pairs[::-1] if flip else pairs)


def limits(mib):
    return pltpu.CompilerParams(vmem_limit_bytes=mib << 20)


def is_direct(n_col):
    return n_col <= MAX_DIRECT and n_col & (n_col - 1) == 0


def shards(n_row, n_col, left_tiles, right, right_index, right_count):
    windows, kept, _, tile = left_tiles.shape
    column_blocks, slots = right.shape[:2]
    part = tile // n_row
    right_count = right_count.reshape(-1)

    if is_direct(n_col):
        shifts = tuple(range(n_col))
        mine = [left_tiles[a] for a in range(windows)]
        gathered = [[None] * n_col for _ in range(windows)]
        for a in range(windows):
            gathered[a][0] = mine[a]
            for k in range(2, n_col, 2):
                gathered[a][k] = exchange(mine[a], "col", n_col, k, flip=a % 2 == 1)
        for a in range(windows):
            for k in range(0, n_col, 2):
                gathered[a][k + 1] = exchange(gathered[a][k], "col", n_col, 1, flip=a % 2 == 1)
    else:
        shifts = (0,)
        whole = lax.all_gather(left_tiles, "col", axis=2, tiled=True)
        gathered = [[whole[a]] for a in range(windows)]

    staged = pl.pallas_call(
        stage_kernel,
        out_shape=jax.ShapeDtypeStruct(right.shape, right.dtype),
        in_specs=[pl.BlockSpec(memory_space=pltpu.HBM)],
        out_specs=VMEM,
        scratch_shapes=[pltpu.SemaphoreType.DMA((column_blocks,))],
        compiler_params=limits(8),
        name="stage",
    )(right)
    sent_rows = column_blocks * part + CODE_ROWS
    multiply = pl.pallas_call(
        functools.partial(product_kernel, n_row, shifts),
        out_shape=[jax.ShapeDtypeStruct((column_blocks, part, tile), jnp.float32)]
        + [jax.ShapeDtypeStruct((sent_rows, tile), jnp.int16)] * (n_row - 1),
        in_specs=[SMEM] * 2 + [VMEM] * (len(shifts) + 1),
        out_specs=[VMEM] * n_row,
        scratch_shapes=[
            pltpu.VMEM((kept + 1, tile, tile), left_tiles.dtype),
            pltpu.VMEM((tile, tile), jnp.float32),
        ],
        cost_estimate=pl.CostEstimate(
            flops=2 * column_blocks * slots * tile**3,
            bytes_accessed=right.size * 2,
            transcendentals=0,
        ),
        compiler_params=limits(16),
        name="product",
    )
    exchanged = []
    for a in range(windows):
        own, *sent = multiply(right_index, right_count, *gathered[a], staged)
        got = [exchange(x, "row", n_row, k + 1, flip=a % 2 == 1) for k, x in enumerate(sent)]
        exchanged.append((own, got))
    squared, sums = [], None
    for a in range(windows):
        own, got = exchanged[a]
        square, sums = pl.pallas_call(
            functools.partial(reduce_kernel, n_row, a > 0),
            out_shape=[
                jax.ShapeDtypeStruct((column_blocks, part, tile), jnp.float32),
                jax.ShapeDtypeStruct((column_blocks, tile), jnp.float32),
            ],
            in_specs=[VMEM] * (n_row + (a > 0)),
            out_specs=[VMEM] * 2,
            compiler_params=limits(8),
            name="reduce",
        )(*got, own, *([sums] if a else []))
        squared.append(square)
    others = [exchange(sums, "row", n_row, k) for k in range(1, n_row)]
    return pl.pallas_call(
        functools.partial(scale_kernel, windows, n_row),
        out_shape=jax.ShapeDtypeStruct((windows, column_blocks, part, tile), jnp.bfloat16),
        in_specs=[VMEM] * (windows + n_row),
        out_specs=VMEM,
        compiler_params=limits(8),
        name="scale",
    )(*squared, sums, *others)


def solution(mesh):
    in_specs = (
        P(None, "row", "col", None),
        P("col", "row", None, None),
        P("col", "row"),
        P("col", "row"),
    )
    out_specs = P(None, "col", "row", None)
    n_row, n_col = mesh.shape["row"], mesh.shape["col"]

    def body(*args):
        return shards(n_row, n_col, *args)

    return jax.shard_map(body, mesh=mesh, in_specs=in_specs, out_specs=out_specs, check_vma=False)
```

profile of v0, /device:TPU:0, one launch (start us, length us, event | category | flops | bytes accessed | tf_op | source)
XLA Modules:
  0.0 54.5 jit_solution(7529075121611345981)
XLA Ops:
  0.0 1.0 %slice_bitcast_fusion = (bf16[8,32,256]{2,1,0:T(8,128)(2,1)S(1)}, bf16[8,32,256]{2,1,0:T(8,128)(2,1)S(1)}) fusion(bf16[2,8,32,256]{3,2,1,0:T(8,128)(2,1)} %param.4), kind=kLoop, calls=%fused_computation | loop fusion | bytes 524288 | tf_op jit(solution)/shard_map/squeeze | solution.py:131
  1.0 3.1 %collective-permute-start.1 = (bf16[8,32,256]{2,1,0:T(8,128)(2,1)S(1)}, bf16[8,32,256]{2,1,0:T(8,128)(2,1)S(1)}, u32[]{:S(2)}, u32[]{:S(2)}) collective-permute-start(bf16[8,32,256]{2,1,0:T(8,128)(2,1)S(1)} %get-tuple-element.30.refs_0_), channel_id=1, source_target_pairs={{0,2},{1,3},{2,0},{3,1},{4,6},{5,7},{6,4},{7,5},{8,10},{9,11},{10,... | collective-permute-start | bytes 393224 | tf_op jit(solution)/shard_map/ppermute | solution.py:112
  4.1 2.6 %collective-permute-start.3 = (bf16[8,32,256]{2,1,0:T(8,128)(2,1)S(1)}, bf16[8,32,256]{2,1,0:T(8,128)(2,1)S(1)}, u32[]{:S(2)}, u32[]{:S(2)}) collective-permute-start(bf16[8,32,256]{2,1,0:T(8,128)(2,1)S(1)} %get-tuple-element.30.refs_0_), channel_id=1, source_target_pairs={{0,4},{1,5},{2,6},{3,7},{4,0},{5,1},{6,2},{7,3},{8,12},{9,13},{10,... | collective-permute-start | bytes 393224 | tf_op jit(solution)/shard_map/ppermute | solution.py:112
  6.7 0.9 %collective-permute-start.11 = (bf16[8,32,256]{2,1,0:T(8,128)(2,1)S(1)}, bf16[8,32,256]{2,1,0:T(8,128)(2,1)S(1)}, u32[]{:S(2)}, u32[]{:S(2)}) collective-permute-start(bf16[8,32,256]{2,1,0:T(8,128)(2,1)S(1)} %get-tuple-element.29.refs_0_), channel_id=1, source_target_pairs={{7,5},{6,4},{5,7},{4,6},{3,1},{2,0},{1,3},{0,2},{15,13},{14,12},{1... | collective-permute-start | bytes 393224 | tf_op jit(solution)/shard_map/ppermute | solution.py:112
  7.6 1.6 %collective-permute-done.1.refs_2_ = bf16[8,32,256]{2,1,0:T(8,128)(2,1)S(1)} collective-permute-done((bf16[8,32,256]{2,1,0:T(8,128)(2,1)S(1)}, bf16[8,32,256]{2,1,0:T(8,128)(2,1)S(1)}, u32[]{:S(2)}, u32[]{:S(2)}) %collective-permute-start.1) | collective-permute-done | bytes 131104 | tf_op jit(solution)/shard_map/ppermute | solution.py:112
  9.2 2.3 %collective-permute-start.13 = (bf16[8,32,256]{2,1,0:T(8,128)(2,1)S(1)}, bf16[8,32,256]{2,1,0:T(8,128)(2,1)S(1)}, u32[]{:S(2)}, u32[]{:S(2)}) collective-permute-start(bf16[8,32,256]{2,1,0:T(8,128)(2,1)S(1)} %get-tuple-element.29.refs_0_), channel_id=1, source_target_pairs={{7,3},{6,2},{5,1},{4,0},{3,7},{2,6},{1,5},{0,4},{15,11},{14,10},{1... | collective-permute-start | bytes 393224 | tf_op jit(solution)/shard_map/ppermute | solution.py:112
  11.5 5.5 %collective-permute-done.3.refs_4_ = bf16[8,32,256]{2,1,0:T(8,128)(2,1)S(1)} collective-permute-done((bf16[8,32,256]{2,1,0:T(8,128)(2,1)S(1)}, bf16[8,32,256]{2,1,0:T(8,128)(2,1)S(1)}, u32[]{:S(2)}, u32[]{:S(2)}) %collective-permute-start.3) | collective-permute-done | bytes 131104 | tf_op jit(solution)/shard_map/ppermute | solution.py:112
  17.0 2.9 %collective-permute-start.15 = (bf16[8,32,256]{2,1,0:T(8,128)(2,1)S(1)}, bf16[8,32,256]{2,1,0:T(8,128)(2,1)S(1)}, u32[]{:S(2)}, u32[]{:S(2)}) collective-permute-start(bf16[8,32,256]{2,1,0:T(8,128)(2,1)S(1)} %get-tuple-element.29.refs_0_), channel_id=1, source_target_pairs={{7,1},{6,0},{5,3},{4,2},{3,5},{2,4},{1,7},{0,6},{15,9},{14,8},{13,... | collective-permute-start | bytes 393224 | tf_op jit(solution)/shard_map/ppermute | solution.py:112
  19.9 0.5 collective-permute-start.4
  20.5 1.9 %copy-done = bf16[4,6,256,256]{3,2,1,0:T(8,128)(2,1)S(1)} copy-done((bf16[4,6,256,256]{3,2,1,0:T(8,128)(2,1)S(1)}, bf16[4,6,256,256]{3,2,1,0:T(8,128)(2,1)}, u32[]{:S(2)}) %copy-start) | copy-done | bytes 3145752
  22.4 0.3 stage.1.refs_8_
  22.7 5.6 %collective-permute-done.13.refs_4_ = bf16[8,32,256]{2,1,0:T(8,128)(2,1)S(1)} collective-permute-done((bf16[8,32,256]{2,1,0:T(8,128)(2,1)S(1)}, bf16[8,32,256]{2,1,0:T(8,128)(2,1)S(1)}, u32[]{:S(2)}, u32[]{:S(2)}) %collective-permute-start.13) | collective-permute-done | bytes 131104 | tf_op jit(solution)/shard_map/ppermute | solution.py:112
  28.2 0.5 collective-permute-start.12
  28.8 0.4 collective-permute-start.16
  29.3 1.8 %product.2 = (f32[4,64,256]{2,1,0:T(8,128)S(1)}, s16[272,256]{1,0:T(8,128)(2,1)S(1)}, s16[272,256]{1,0:T(8,128)(2,1)S(1)}, s16[272,256]{1,0:T(8,128)(2,1)S(1)}) custom-call(s32[4,6]{1,0:T(4,128)S(1)} %copy-done.1, s32[4]{0:T(128)S(1)} %bitcast.5, bf16[8,32,256]{2,1,0:T(8,128)(2,1)S(1)} %get-tuple-element.30.refs_0_, ...), custom_call_target="tpu_custom_call" | custom-call | flops 805306368 | bytes 3145728 | tf_op jit(solution)/shard_map/product/pallas_call | solution.py:175
  31.1 1.6 %collective-permute-start.7 = (s16[272,256]{1,0:T(8,128)(2,1)S(1)}, s16[272,256]{1,0:T(8,128)(2,1)S(1)}, u32[]{:S(2)}, u32[]{:S(2)}) collective-permute-start(s16[272,256]{1,0:T(8,128)(2,1)S(1)} %get-tuple-element.17), channel_id=1, source_target_pairs={{0,8},{8,0},{16,24},{24,16},{1,9},{9,1},{17,25},{25,17},{2,10},{10... | collective-permute-start | bytes 417800 | tf_op jit(solution)/shard_map/ppermute | solution.py:112
  32.6 1.5 %collective-permute-start.8 = (s16[272,256]{1,0:T(8,128)(2,1)S(1)}, s16[272,256]{1,0:T(8,128)(2,1)S(1)}, u32[]{:S(2)}, u32[]{:S(2)}) collective-permute-start(s16[272,256]{1,0:T(8,128)(2,1)S(1)} %get-tuple-element.18), channel_id=1, source_target_pairs={{0,16},{8,24},{16,0},{24,8},{1,17},{9,25},{17,1},{25,9},{2,18},{10... | collective-permute-start | bytes 417800 | tf_op jit(solution)/shard_map/ppermute | solution.py:112
  34.2 0.5 collective-permute-start.9
  34.6 1.8 %product.3 = (f32[4,64,256]{2,1,0:T(8,128)S(1)}, s16[272,256]{1,0:T(8,128)(2,1)S(1)}, s16[272,256]{1,0:T(8,128)(2,1)S(1)}, s16[272,256]{1,0:T(8,128)(2,1)S(1)}) custom-call(s32[4,6]{1,0:T(4,128)S(1)} %copy-done.1, s32[4]{0:T(128)S(1)} %bitcast.6, bf16[8,32,256]{2,1,0:T(8,128)(2,1)S(1)} %get-tuple-element.29.refs_0_, ...), custom_call_target="tpu_custom_call" | custom-call | flops 805306368 | bytes 3145728 | tf_op jit(solution)/shard_map/product/pallas_call | solution.py:175
  36.4 1.6 %collective-permute-start.17 = (s16[272,256]{1,0:T(8,128)(2,1)S(1)}, s16[272,256]{1,0:T(8,128)(2,1)S(1)}, u32[]{:S(2)}, u32[]{:S(2)}) collective-permute-start(s16[272,256]{1,0:T(8,128)(2,1)S(1)} %get-tuple-element.22), channel_id=1, source_target_pairs={{24,16},{16,24},{8,0},{0,8},{25,17},{17,25},{9,1},{1,9},{26,18},{1... | collective-permute-start | bytes 417800 | tf_op jit(solution)/shard_map/ppermute | solution.py:112
  38.0 1.5 %collective-permute-start.18 = (s16[272,256]{1,0:T(8,128)(2,1)S(1)}, s16[272,256]{1,0:T(8,128)(2,1)S(1)}, u32[]{:S(2)}, u32[]{:S(2)}) collective-permute-start(s16[272,256]{1,0:T(8,128)(2,1)S(1)} %get-tuple-element.23), channel_id=1, source_target_pairs={{24,8},{16,0},{8,24},{0,16},{25,9},{17,1},{9,25},{1,17},{26,10},{1... | collective-permute-start | bytes 417800 | tf_op jit(solution)/shard_map/ppermute | solution.py:112
  39.5 0.6 %collective-permute-start.19 = (s16[272,256]{1,0:T(8,128)(2,1)S(1)}, s16[272,256]{1,0:T(8,128)(2,1)S(1)}, u32[]{:S(2)}, u32[]{:S(2)}) collective-permute-start(s16[272,256]{1,0:T(8,128)(2,1)S(1)} %get-tuple-element.24), channel_id=1, source_target_pairs={{24,0},{16,8},{8,16},{0,24},{25,1},{17,9},{9,17},{1,25},{26,2},{18... | collective-permute-start | bytes 417800 | tf_op jit(solution)/shard_map/ppermute | solution.py:112
  40.1 0.8 %collective-permute-done.8.refs_1_ = s16[272,256]{1,0:T(8,128)(2,1)S(1)} collective-permute-done((s16[272,256]{1,0:T(8,128)(2,1)S(1)}, s16[272,256]{1,0:T(8,128)(2,1)S(1)}, u32[]{:S(2)}, u32[]{:S(2)}) %collective-permute-start.8) | collective-permute-done | bytes 139296 | tf_op jit(solution)/shard_map/ppermute | solution.py:112
  40.9 0.7 %collective-permute-done.9.refs_2_ = s16[272,256]{1,0:T(8,128)(2,1)S(1)} collective-permute-done((s16[272,256]{1,0:T(8,128)(2,1)S(1)}, s16[272,256]{1,0:T(8,128)(2,1)S(1)}, u32[]{:S(2)}, u32[]{:S(2)}) %collective-permute-start.9) | collective-permute-done | bytes 139296 | tf_op jit(solution)/shard_map/ppermute | solution.py:112
  41.8 1.8 %collective-permute-done.17.refs_0_ = s16[272,256]{1,0:T(8,128)(2,1)S(1)} collective-permute-done((s16[272,256]{1,0:T(8,128)(2,1)S(1)}, s16[272,256]{1,0:T(8,128)(2,1)S(1)}, u32[]{:S(2)}, u32[]{:S(2)}) %collective-permute-start.17) | collective-permute-done | bytes 139296 | tf_op jit(solution)/shard_map/ppermute | solution.py:112
  43.7 3.3 %collective-permute-done.18.refs_1_ = s16[272,256]{1,0:T(8,128)(2,1)S(1)} collective-permute-done((s16[272,256]{1,0:T(8,128)(2,1)S(1)}, s16[272,256]{1,0:T(8,128)(2,1)S(1)}, u32[]{:S(2)}, u32[]{:S(2)}) %collective-permute-start.18) | collective-permute-done | bytes 139296 | tf_op jit(solution)/shard_map/ppermute | solution.py:112
  47.1 1.3 %collective-permute-start.20 = (f32[4,256]{1,0:T(4,128)S(1)}, f32[4,256]{1,0:T(4,128)S(1)}, u32[]{:S(2)}, u32[]{:S(2)}) collective-permute-start(f32[4,256]{1,0:T(4,128)S(1)} %get-tuple-element.28.refs_2_), channel_id=1, source_target_pairs={{0,8},{8,0},{16,24},{24,16},{1,9},{9,1},{17,25},{25,17},{2,10},{10... | collective-permute-start | bytes 12296 | tf_op jit(solution)/shard_map/ppermute | solution.py:112
  48.5 0.8 %collective-permute-start.21 = (f32[4,256]{1,0:T(4,128)S(1)}, f32[4,256]{1,0:T(4,128)S(1)}, u32[]{:S(2)}, u32[]{:S(2)}) collective-permute-start(f32[4,256]{1,0:T(4,128)S(1)} %get-tuple-element.28.refs_2_), channel_id=1, source_target_pairs={{0,16},{8,24},{16,0},{24,8},{1,17},{9,25},{17,1},{25,9},{2,18},{10... | collective-permute-start | bytes 12296 | tf_op jit(solution)/shard_map/ppermute | solution.py:112
  49.3 1.4 %collective-permute-start.22 = (f32[4,256]{1,0:T(4,128)S(1)}, f32[4,256]{1,0:T(4,128)S(1)}, u32[]{:S(2)}, u32[]{:S(2)}) collective-permute-start(f32[4,256]{1,0:T(4,128)S(1)} %get-tuple-element.28.refs_2_), channel_id=1, source_target_pairs={{0,24},{8,16},{16,8},{24,0},{1,25},{9,17},{17,9},{25,1},{2,26},{10... | collective-permute-start | bytes 12296 | tf_op jit(solution)/shard_map/ppermute | solution.py:112
  50.8 1.3 %collective-permute-done.21.refs_4_ = f32[4,256]{1,0:T(4,128)S(1)} collective-permute-done((f32[4,256]{1,0:T(4,128)S(1)}, f32[4,256]{1,0:T(4,128)S(1)}, u32[]{:S(2)}, u32[]{:S(2)}) %collective-permute-start.21) | collective-permute-done | bytes 4128 | tf_op jit(solution)/shard_map/ppermute | solution.py:112
  52.1 1.7 %collective-permute-done.22.refs_5_ = f32[4,256]{1,0:T(4,128)S(1)} collective-permute-done((f32[4,256]{1,0:T(4,128)S(1)}, f32[4,256]{1,0:T(4,128)S(1)}, u32[]{:S(2)}, u32[]{:S(2)}) %collective-permute-start.22) | collective-permute-done | bytes 4128 | tf_op jit(solution)/shard_map/ppermute | solution.py:112
  53.8 0.7 %scale.1 = bf16[2,4,64,256]{3,2,1,0:T(8,128)(2,1)} custom-call(f32[4,64,256]{2,1,0:T(8,128)S(1)} %get-tuple-element.21.refs_0_, f32[4,64,256]{2,1,0:T(8,128)S(1)} %get-tuple-element.27.refs_1_, f32[4,256]{1,0:T(4,128)S(1)} %get-tuple-element.28.refs_2_, f32[4,256]{1,0:T(4,128)S(1)} %collective-permute-done.20.refs_3_, ...), custom_call_target="tpu_custom_call" | custom-call | tf_op jit(solution)/shard_map/scale/pallas_call | solution.py:194
  (27 shorter events, 0.7 us)
Async XLA Ops:
  1.0 28.3 %copy-start.1 = (s32[4,6]{1,0:T(4,128)S(1)}, s32[4,6]{1,0:T(4,128)}, u32[]{:S(2)}) copy-start(s32[4,6]{1,0:T(4,128)} %index_ref.3) | copy-start | bytes 292
  1.0 8.2 %collective-permute-start.1 = (bf16[8,32,256]{2,1,0:T(8,128)(2,1)S(1)}, bf16[8,32,256]{2,1,0:T(8,128)(2,1)S(1)}, u32[]{:S(2)}, u32[]{:S(2)}) collective-permute-start(bf16[8,32,256]{2,1,0:T(8,128)(2,1)S(1)} %get-tuple-element.30.refs_0_), channel_id=1, source_target_pairs={{0,2},{1,3},{2,0},{3,1},{4,6},{5,7},{6,4},{7,5},{8,10},{9,11},{10,... | collective-permute-start | bytes 393224 | tf_op jit(solution)/shard_map/ppermute | solution.py:112
  4.1 12.9 %collective-permute-start.3 = (bf16[8,32,256]{2,1,0:T(8,128)(2,1)S(1)}, bf16[8,32,256]{2,1,0:T(8,128)(2,1)S(1)}, u32[]{:S(2)}, u32[]{:S(2)}) collective-permute-start(bf16[8,32,256]{2,1,0:T(8,128)(2,1)S(1)} %get-tuple-element.30.refs_0_), channel_id=1, source_target_pairs={{0,4},{1,5},{2,6},{3,7},{4,0},{5,1},{6,2},{7,3},{8,12},{9,13},{10,... | collective-permute-start | bytes 393224 | tf_op jit(solution)/shard_map/ppermute | solution.py:112
  6.7 13.2 %collective-permute-start.5 = (bf16[8,32,256]{2,1,0:T(8,128)(2,1)S(1)}, bf16[8,32,256]{2,1,0:T(8,128)(2,1)S(1)}, u32[]{:S(2)}, u32[]{:S(2)}) collective-permute-start(bf16[8,32,256]{2,1,0:T(8,128)(2,1)S(1)} %get-tuple-element.30.refs_0_), channel_id=1, source_target_pairs={{0,6},{1,7},{2,4},{3,5},{4,2},{5,3},{6,0},{7,1},{8,14},{9,15},{10,... | collective-permute-start | bytes 393224 | tf_op jit(solution)/shard_map/ppermute | solution.py:112
  6.7 13.2 %collective-permute-start = (bf16[8,32,256]{2,1,0:T(8,128)(2,1)S(1)}, bf16[8,32,256]{2,1,0:T(8,128)(2,1)S(1)}, u32[]{:S(2)}, u32[]{:S(2)}) collective-permute-start(bf16[8,32,256]{2,1,0:T(8,128)(2,1)S(1)} %get-tuple-element.30.refs_0_), channel_id=1, source_target_pairs={{0,1},{1,0},{2,3},{3,2},{4,5},{5,4},{6,7},{7,6},{8,9},{9,8},{10,11... | collective-permute-start | bytes 393224 | tf_op jit(solution)/shard_map/ppermute | solution.py:112
  6.7 22.6 %copy-start.2 = (s32[4,1]{0,1:T(1,128)S(1)}, s32[4,1]{0,1:T(1,128)}, u32[]{:S(2)}) copy-start(s32[4,1]{0,1:T(1,128)} %param.7) | copy-start | bytes 52
  6.7 13.7 %collective-permute-start.11 = (bf16[8,32,256]{2,1,0:T(8,128)(2,1)S(1)}, bf16[8,32,256]{2,1,0:T(8,128)(2,1)S(1)}, u32[]{:S(2)}, u32[]{:S(2)}) collective-permute-start(bf16[8,32,256]{2,1,0:T(8,128)(2,1)S(1)} %get-tuple-element.29.refs_0_), channel_id=1, source_target_pairs={{7,5},{6,4},{5,7},{4,6},{3,1},{2,0},{1,3},{0,2},{15,13},{14,12},{1... | collective-permute-start | bytes 393224 | tf_op jit(solution)/shard_map/ppermute | solution.py:112
  9.2 19.0 %collective-permute-start.13 = (bf16[8,32,256]{2,1,0:T(8,128)(2,1)S(1)}, bf16[8,32,256]{2,1,0:T(8,128)(2,1)S(1)}, u32[]{:S(2)}, u32[]{:S(2)}) collective-permute-start(bf16[8,32,256]{2,1,0:T(8,128)(2,1)S(1)} %get-tuple-element.29.refs_0_), channel_id=1, source_target_pairs={{7,3},{6,2},{5,1},{4,0},{3,7},{2,6},{1,5},{0,4},{15,11},{14,10},{1... | collective-permute-start | bytes 393224 | tf_op jit(solution)/shard_map/ppermute | solution.py:112
  17.0 11.2 %collective-permute-start.15 = (bf16[8,32,256]{2,1,0:T(8,128)(2,1)S(1)}, bf16[8,32,256]{2,1,0:T(8,128)(2,1)S(1)}, u32[]{:S(2)}, u32[]{:S(2)}) collective-permute-start(bf16[8,32,256]{2,1,0:T(8,128)(2,1)S(1)} %get-tuple-element.29.refs_0_), channel_id=1, source_target_pairs={{7,1},{6,0},{5,3},{4,2},{3,5},{2,4},{1,7},{0,6},{15,9},{14,8},{13,... | collective-permute-start | bytes 393224 | tf_op jit(solution)/shard_map/ppermute | solution.py:112
  19.9 8.8 %collective-permute-start.2 = (bf16[8,32,256]{2,1,0:T(8,128)(2,1)S(1)}, bf16[8,32,256]{2,1,0:T(8,128)(2,1)S(1)}, u32[]{:S(2)}, u32[]{:S(2)}) collective-permute-start(bf16[8,32,256]{2,1,0:T(8,128)(2,1)S(1)} %collective-permute-done.1.refs_2_), channel_id=1, source_target_pairs={{0,1},{1,0},{2,3},{3,2},{4,5},{5,4},{6,7},{7,6},{8,9},{9,8},{10,11... | collective-permute-start | bytes 393224 | tf_op jit(solution)/shard_map/ppermute | solution.py:112
  19.9 8.9 %collective-permute-start.4 = (bf16[8,32,256]{2,1,0:T(8,128)(2,1)S(1)}, bf16[8,32,256]{2,1,0:T(8,128)(2,1)S(1)}, u32[]{:S(2)}, u32[]{:S(2)}) collective-permute-start(bf16[8,32,256]{2,1,0:T(8,128)(2,1)S(1)} %collective-permute-done.3.refs_4_), channel_id=1, source_target_pairs={{0,1},{1,0},{2,3},{3,2},{4,5},{5,4},{6,7},{7,6},{8,9},{9,8},{10,11... | collective-permute-start | bytes 393224 | tf_op jit(solution)/shard_map/ppermute | solution.py:112
  20.4 8.8 %collective-permute-start.6 = (bf16[8,32,256]{2,1,0:T(8,128)(2,1)S(1)}, bf16[8,32,256]{2,1,0:T(8,128)(2,1)S(1)}, u32[]{:S(2)}, u32[]{:S(2)}) collective-permute-start(bf16[8,32,256]{2,1,0:T(8,128)(2,1)S(1)} %collective-permute-done.5.refs_6_), channel_id=1, source_target_pairs={{0,1},{1,0},{2,3},{3,2},{4,5},{5,4},{6,7},{7,6},{8,9},{9,8},{10,11... | collective-permute-start | bytes 393224 | tf_op jit(solution)/shard_map/ppermute | solution.py:112
  20.5 1.9 %copy-start = (bf16[4,6,256,256]{3,2,1,0:T(8,128)(2,1)S(1)}, bf16[4,6,256,256]{3,2,1,0:T(8,128)(2,1)}, u32[]{:S(2)}) copy-start(bf16[4,6,256,256]{3,2,1,0:T(8,128)(2,1)} %right_ref.1) | copy-start | bytes 9437188
  28.2 4.4 %collective-permute-start.10 = (bf16[8,32,256]{2,1,0:T(8,128)(2,1)S(1)}, bf16[8,32,256]{2,1,0:T(8,128)(2,1)S(1)}, u32[]{:S(2)}, u32[]{:S(2)}) collective-permute-start(bf16[8,32,256]{2,1,0:T(8,128)(2,1)S(1)} %get-tuple-element.29.refs_0_), channel_id=1, source_target_pairs={{7,6},{6,7},{5,4},{4,5},{3,2},{2,3},{1,0},{0,1},{15,14},{14,15},{1... | collective-permute-start | bytes 393224 | tf_op jit(solution)/shard_map/ppermute | solution.py:112
  28.2 5.9 %collective-permute-start.12 = (bf16[8,32,256]{2,1,0:T(8,128)(2,1)S(1)}, bf16[8,32,256]{2,1,0:T(8,128)(2,1)S(1)}, u32[]{:S(2)}, u32[]{:S(2)}) collective-permute-start(bf16[8,32,256]{2,1,0:T(8,128)(2,1)S(1)} %collective-permute-done.11.refs_2_), channel_id=1, source_target_pairs={{7,6},{6,7},{5,4},{4,5},{3,2},{2,3},{1,0},{0,1},{15,14},{14,15},{1... | collective-permute-start | bytes 393224 | tf_op jit(solution)/shard_map/ppermute | solution.py:112
  28.8 5.9 %collective-permute-start.14 = (bf16[8,32,256]{2,1,0:T(8,128)(2,1)S(1)}, bf16[8,32,256]{2,1,0:T(8,128)(2,1)S(1)}, u32[]{:S(2)}, u32[]{:S(2)}) collective-permute-start(bf16[8,32,256]{2,1,0:T(8,128)(2,1)S(1)} %collective-permute-done.13.refs_4_), channel_id=1, source_target_pairs={{7,6},{6,7},{5,4},{4,5},{3,2},{2,3},{1,0},{0,1},{15,14},{14,15},{1... | collective-permute-start | bytes 393224 | tf_op jit(solution)/shard_map/ppermute | solution.py:112
  28.8 5.8 %collective-permute-start.16 = (bf16[8,32,256]{2,1,0:T(8,128)(2,1)S(1)}, bf16[8,32,256]{2,1,0:T(8,128)(2,1)S(1)}, u32[]{:S(2)}, u32[]{:S(2)}) collective-permute-start(bf16[8,32,256]{2,1,0:T(8,128)(2,1)S(1)} %collective-permute-done.15.refs_6_), channel_id=1, source_target_pairs={{7,6},{6,7},{5,4},{4,5},{3,2},{2,3},{1,0},{0,1},{15,14},{14,15},{1... | collective-permute-start | bytes 393224 | tf_op jit(solution)/shard_map/ppermute | solution.py:112
  31.1 8.4 %collective-permute-start.7 = (s16[272,256]{1,0:T(8,128)(2,1)S(1)}, s16[272,256]{1,0:T(8,128)(2,1)S(1)}, u32[]{:S(2)}, u32[]{:S(2)}) collective-permute-start(s16[272,256]{1,0:T(8,128)(2,1)S(1)} %get-tuple-element.17), channel_id=1, source_target_pairs={{0,8},{8,0},{16,24},{24,16},{1,9},{9,1},{17,25},{25,17},{2,10},{10... | collective-permute-start | bytes 417800 | tf_op jit(solution)/shard_map/ppermute | solution.py:112
  32.6 8.3 %collective-permute-start.8 = (s16[272,256]{1,0:T(8,128)(2,1)S(1)}, s16[272,256]{1,0:T(8,128)(2,1)S(1)}, u32[]{:S(2)}, u32[]{:S(2)}) collective-permute-start(s16[272,256]{1,0:T(8,128)(2,1)S(1)} %get-tuple-element.18), channel_id=1, source_target_pairs={{0,16},{8,24},{16,0},{24,8},{1,17},{9,25},{17,1},{25,9},{2,18},{10... | collective-permute-start | bytes 417800 | tf_op jit(solution)/shard_map/ppermute | solution.py:112
  34.2 7.5 %collective-permute-start.9 = (s16[272,256]{1,0:T(8,128)(2,1)S(1)}, s16[272,256]{1,0:T(8,128)(2,1)S(1)}, u32[]{:S(2)}, u32[]{:S(2)}) collective-permute-start(s16[272,256]{1,0:T(8,128)(2,1)S(1)} %get-tuple-element.19), channel_id=1, source_target_pairs={{0,24},{8,16},{16,8},{24,0},{1,25},{9,17},{17,9},{25,1},{2,26},{10... | collective-permute-start | bytes 417800 | tf_op jit(solution)/shard_map/ppermute | solution.py:112
  36.4 7.2 %collective-permute-start.17 = (s16[272,256]{1,0:T(8,128)(2,1)S(1)}, s16[272,256]{1,0:T(8,128)(2,1)S(1)}, u32[]{:S(2)}, u32[]{:S(2)}) collective-permute-start(s16[272,256]{1,0:T(8,128)(2,1)S(1)} %get-tuple-element.22), channel_id=1, source_target_pairs={{24,16},{16,24},{8,0},{0,8},{25,17},{17,25},{9,1},{1,9},{26,18},{1... | collective-permute-start | bytes 417800 | tf_op jit(solution)/shard_map/ppermute | solution.py:112
  38.0 9.0 %collective-permute-start.18 = (s16[272,256]{1,0:T(8,128)(2,1)S(1)}, s16[272,256]{1,0:T(8,128)(2,1)S(1)}, u32[]{:S(2)}, u32[]{:S(2)}) collective-permute-start(s16[272,256]{1,0:T(8,128)(2,1)S(1)} %get-tuple-element.23), channel_id=1, source_target_pairs={{24,8},{16,0},{8,24},{0,16},{25,9},{17,1},{9,25},{1,17},{26,10},{1... | collective-permute-start | bytes 417800 | tf_op jit(solution)/shard_map/ppermute | solution.py:112
  39.5 7.4 %collective-permute-start.19 = (s16[272,256]{1,0:T(8,128)(2,1)S(1)}, s16[272,256]{1,0:T(8,128)(2,1)S(1)}, u32[]{:S(2)}, u32[]{:S(2)}) collective-permute-start(s16[272,256]{1,0:T(8,128)(2,1)S(1)} %get-tuple-element.24), channel_id=1, source_target_pairs={{24,0},{16,8},{8,16},{0,24},{25,1},{17,9},{9,17},{1,25},{26,2},{18... | collective-permute-start | bytes 417800 | tf_op jit(solution)/shard_map/ppermute | solution.py:112
  47.1 3.7 %collective-permute-start.20 = (f32[4,256]{1,0:T(4,128)S(1)}, f32[4,256]{1,0:T(4,128)S(1)}, u32[]{:S(2)}, u32[]{:S(2)}) collective-permute-start(f32[4,256]{1,0:T(4,128)S(1)} %get-tuple-element.28.refs_2_), channel_id=1, source_target_pairs={{0,8},{8,0},{16,24},{24,16},{1,9},{9,1},{17,25},{25,17},{2,10},{10... | collective-permute-start | bytes 12296 | tf_op jit(solution)/shard_map/ppermute | solution.py:112
  48.5 3.6 %collective-permute-start.21 = (f32[4,256]{1,0:T(4,128)S(1)}, f32[4,256]{1,0:T(4,128)S(1)}, u32[]{:S(2)}, u32[]{:S(2)}) collective-permute-start(f32[4,256]{1,0:T(4,128)S(1)} %get-tuple-element.28.refs_2_), channel_id=1, source_target_pairs={{0,16},{8,24},{16,0},{24,8},{1,17},{9,25},{17,1},{25,9},{2,18},{10... | collective-permute-start | bytes 12296 | tf_op jit(solution)/shard_map/ppermute | solution.py:112
  49.3 4.5 %collective-permute-start.22 = (f32[4,256]{1,0:T(4,128)S(1)}, f32[4,256]{1,0:T(4,128)S(1)}, u32[]{:S(2)}, u32[]{:S(2)}) collective-permute-start(f32[4,256]{1,0:T(4,128)S(1)} %get-tuple-element.28.refs_2_), channel_id=1, source_target_pairs={{0,24},{8,16},{16,8},{24,0},{1,25},{9,17},{17,9},{25,1},{2,26},{10... | collective-permute-start | bytes 12296 | tf_op jit(solution)/shard_map/ppermute | solution.py:112
where the time goes:
time: 54.7 us; the launch traced here: 54.5 us
  starting transfers between devices  24.2 us (44%)
  waiting for transfers between devices  22.4 us (41%)
  Pallas kernels  4.91 us (9%)
  local copies, waits for them, and re-layouts  2.88 us (5%)
    ppermute x23, starting transfers between devices, exchange(): return lax.ppermute(x, axis, pairs[::-1] if flip else pairs)  24.2 us
    ppermute x23, waiting for transfers between devices, exchange(): return lax.ppermute(x, axis, pairs[::-1] if flip else pairs)  22.4 us
    pallas_call x2, Pallas kernels, shards(): own, *sent = multiply(right_index, right_count, *gathered[a], staged)  3.56 us
    unnamed x6, local copies, waits for them, and re-layouts  1.9 us
  transfers between devices with their start and end apart: 23, of which 10 were waited for; matrix products, arithmetic and copies ran while one was open for 0% of the time, Pallas kernels for 7%

commit v1 on v0

--- a/solution.py
+++ b/solution.py
@@ -11,7 +11,6 @@
 OFFSET = 32640
 LOG_STEPS = 256.0
 CODE_ROWS = 16
-MAX_DIRECT = 8
 
 VMEM = pl.BlockSpec(memory_space=pltpu.VMEM)
 SMEM = pl.BlockSpec(memory_space=pltpu.SMEM)
@@ -28,7 +27,7 @@
         copy.wait()
 
 
-def product_kernel(n_row, shifts, index_ref, count_ref, *refs):
+def product_kernel(n_row, window, shifts, index_ref, count_ref, *refs):
     n_block = len(shifts)
     blocks, right_ref = refs[:n_block], refs[n_block]
     own_ref = refs[n_block + 1]
@@ -38,13 +37,23 @@
     kept = left.shape[0] - 1
     part = tile // n_row
     row = lax.axis_index("row")
-    for block, shift in zip(blocks, shifts):
+    for block, (shift, ends) in zip(blocks, shifts):
+        if block.ndim == 4:
+            block = block.at[window]
         rows = block.shape[1]
-        if n_block == 1:
+        if rows == tile:
             left[:kept] = block[...]
+            continue
+        col = lax.axis_index("col")
+        start = pl.multiple_of((col ^ shift) * rows, rows)
+
+        def place(block=block, start=start, rows=rows):
+            left[:kept, pl.ds(start, rows), :] = block[...]
+
+        if ends is None:
+            place()
         else:
-            start = pl.multiple_of((lax.axis_index("col") ^ shift) * rows, rows)
-            left[:kept, pl.ds(start, rows), :] = block[...]
+            pl.when(is_end(col, tile // rows) == ends)(place)
     left[kept] = jnp.zeros(left.shape[1:], left.dtype)
     lines = lax.broadcasted_iota(jnp.int32, (CODE_ROWS, tile), 0)
     codes = jnp.zeros((CODE_ROWS, tile), jnp.int32)
@@ -116,8 +125,16 @@
     return pltpu.CompilerParams(vmem_limit_bytes=mib << 20)
 
 
+def is_end(col, n_col):
+    return (col < 2) | (col >= n_col - 2)
+
+
+def pairs_of(moves):
+    return [(2 * i + c, 2 * j + c) for i, j in moves for c in (0, 1)]
+
+
 def is_direct(n_col):
-    return n_col <= MAX_DIRECT and n_col & (n_col - 1) == 0
+    return n_col == 8
 
 
 def shards(n_row, n_col, left_tiles, right, right_index, right_count):
@@ -127,20 +144,33 @@
     right_count = right_count.reshape(-1)
 
     if is_direct(n_col):
-        shifts = tuple(range(n_col))
-        mine = [left_tiles[a] for a in range(windows)]
-        gathered = [[None] * n_col for _ in range(windows)]
+        swap = [(i, i ^ 1) for i in range(n_col)]
+        ends = [p for p in swap if p[0] < 2 or p[0] >= n_col - 2]
+        inner = [p for p in swap if p not in ends]
+        halves = [left_tiles[0]]
+        halves += [x[a] for a, x in [(1, lax.optimization_barrier(left_tiles))]]
+        far, middle, gathered = [], [], []
         for a in range(windows):
-            gathered[a][0] = mine[a]
-            for k in range(2, n_col, 2):
-                gathered[a][k] = exchange(mine[a], "col", n_col, k, flip=a % 2 == 1)
+            flip = -1 if a % 2 else 1
+            far.append(lax.ppermute(halves[a], "col", [(i, i ^ 4) for i in range(n_col)][::flip]))
+            middle.append(lax.ppermute(halves[a], "col", pairs_of([(1, 2), (2, 1)])[::flip]))
+        beside = lax.ppermute(left_tiles, "col", [(i, i ^ 2) for i in range(n_col)])
+        pair = lax.ppermute(left_tiles, "col", swap)
+        beside_pair = lax.ppermute(beside, "col", swap[::-1])
+        shifts = ((0, None), (1, None), (2, None), (3, None), (4, None), (5, None))
+        shifts += ((6, False), (7, False), (6, True), (7, True))
         for a in range(windows):
-            for k in range(0, n_col, 2):
-                gathered[a][k + 1] = exchange(gathered[a][k], "col", n_col, 1, flip=a % 2 == 1)
+            flip = -1 if a % 2 else 1
+            relay = lax.ppermute(far[a], "col", pairs_of([(1, 0), (2, 3)])[::flip])
+            blocks = [left_tiles, pair, beside, beside_pair, far[a]]
+            blocks.append(lax.ppermute(far[a], "col", swap[::flip]))
+            blocks += [middle[a], lax.ppermute(middle[a], "col", inner[::flip])]
+            blocks += [relay, lax.ppermute(relay, "col", ends[::flip])]
+            gathered.append(blocks)
     else:
-        shifts = (0,)
+        shifts = ((0, None),)
         whole = lax.all_gather(left_tiles, "col", axis=2, tiled=True)
-        gathered = [[whole[a]] for a in range(windows)]
+        gathered = [[whole]] * windows
 
     staged = pl.pallas_call(
         stage_kernel,
@@ -152,8 +182,8 @@
         name="stage",
     )(right)
     sent_rows = column_blocks * part + CODE_ROWS
-    multiply = pl.pallas_call(
-        functools.partial(product_kernel, n_row, shifts),
+    multiply = lambda a: pl.pallas_call(
+        functools.partial(product_kernel, n_row, a, shifts),
         out_shape=[jax.ShapeDtypeStruct((column_blocks, part, tile), jnp.float32)]
         + [jax.ShapeDtypeStruct((sent_rows, tile), jnp.int16)] * (n_row - 1),
         in_specs=[SMEM] * 2 + [VMEM] * (len(shifts) + 1),
@@ -172,7 +202,7 @@
     )
     exchanged = []
     for a in range(windows):
-        own, *sent = multiply(right_index, right_count, *gathered[a], staged)
+        own, *sent = multiply(a)(right_index, right_count, *gathered[a], staged)
         got = [exchange(x, "row", n_row, k + 1, flip=a % 2 == 1) for k, x in enumerate(sent)]
         exchanged.append((own, got))
     squared, sums = [], None

time: 54.7 us -> 61.1 us (1.12)
  starting transfers between devices: 24.2 us -> 32 us
  waiting for transfers between devices: 22.4 us -> 19.8 us
  local copies, waits for them, and re-layouts: 2.88 us -> 3.82 us
    ppermute x0 -> x15, starting transfers between devices: none -> 19 us  [the longest x2 5.87 us: shards(): lax.ppermute(halves[a], 'col', [(i, i ^ 4) for i in range(n_col)][::flip])]
    ppermute x23 -> x9, waiting for transfers between devices: 22.4 us -> 8.86 us  [exchange(): return lax.ppermute(x, axis, pairs[::-1] if flip else pairs)]
    ppermute x23 -> x9, starting transfers between devices: 24.2 us -> 13 us  [exchange(): return lax.ppermute(x, axis, pairs[::-1] if flip else pairs)]
    ppermute x0 -> x15, waiting for transfers between devices: none -> 11 us  [the longest x2 9.05 us: shards(): lax.ppermute(halves[a], 'col', [(i, i ^ 4) for i in range(n_col)][::flip])]
    squeeze x1 -> x2, local copies, waits for them, and re-layouts: 0.98 us -> 1.92 us  [the longest x1 0.98 us: shards(): halves += [x[a] for a, x in [(1, lax.optimization_barrier(left_tiles))]]]
    unnamed x6 -> x8, local copies, waits for them, and re-layouts: 1.9 us -> 1.9 us
  transfers between devices with their start and end apart: 23 -> 24, of which waited for: 10 -> 10; matrix products, arithmetic and copies ran while one was open for 0% -> 3% of each run, Pallas kernels for 7% -> 7%
where the time goes in v1:
time: 61.1 us; the launch traced here: 60.8 us
  starting transfers between devices  32 us (52%)
  waiting for transfers between devices  19.8 us (32%)
  Pallas kernels  4.96 us (8%)
  local copies, waits for them, and re-layouts  3.82 us (6%)
    ppermute x9, starting transfers between devices, exchange(): return lax.ppermute(x, axis, pairs[::-1] if flip else pairs)  13 us
    ppermute x2, waiting for transfers between devices, shards(): lax.ppermute(halves[a], 'col', [(i, i ^ 4) for i in range(n_col)][::flip])  9.05 us
    ppermute x9, waiting for transfers between devices, exchange(): return lax.ppermute(x, axis, pairs[::-1] if flip else pairs)  8.86 us
    ppermute x2, starting transfers between devices, shards(): lax.ppermute(halves[a], 'col', [(i, i ^ 4) for i in range(n_col)][::flip])  5.87 us
    ppermute x2, starting transfers between devices, shards(): blocks += [relay, lax.ppermute(relay, 'col', ends[::flip])]  3.83 us
    pallas_call x2, Pallas kernels, shards(): own, *sent = multiply(a)(right_index, right_count, *gathered[a], staged)  3.61 us
    ppermute x1, starting transfers between devices, shards(): beside = lax.ppermute(left_tiles, 'col', [(i, i ^ 2) for i in range(n_col)])  3.05 us
    ppermute x2, starting transfers between devices, shards(): relay = lax.ppermute(far[a], 'col', pairs_of([(1, 0), (2, 3)])[::flip])  2.56 us
  transfers between devices with their start and end apart: 24, of which 10 were waited for; matrix products, arithmetic and copies ran while one was open for 3% of the time, Pallas kernels for 7%

profile of v1, /device:TPU:0, one launch (start us, length us, event | category | flops | bytes accessed | tf_op | source)
XLA Modules:
  0.0 60.8 jit_solution(16101115264471613786)
XLA Ops:
  0.0 3.1 %collective-permute-start.1 = (bf16[2,8,32,256]{3,2,1,0:T(8,128)(2,1)}, bf16[2,8,32,256]{3,2,1,0:T(8,128)(2,1)S(1)}, u32[]{:S(2)}, u32[]{:S(2)}) collective-permute-start(bf16[2,8,32,256]{3,2,1,0:T(8,128)(2,1)} %refs_0_.3), channel_id=1, source_target_pairs={{0,2},{1,3},{2,0},{3,1},{4,6},{5,7},{6,4},{7,5},{8,10},{9,11},{10,... | collective-permute-start | bytes 786440 | tf_op jit(solution)/shard_map/ppermute | solution.py:157
  3.1 0.9 %slice_bitcast_fusion.1 = bf16[8,32,256]{2,1,0:T(8,128)(2,1)S(1)} fusion(bf16[2,8,32,256]{3,2,1,0:T(8,128)(2,1)} %refs_0_.3), kind=kLoop, calls=%fused_computation.1 | loop fusion | bytes 262144 | tf_op jit(solution)/shard_map/squeeze | solution.py:150
  4.0 2.7 %collective-permute-start.3 = (bf16[8,32,256]{2,1,0:T(8,128)(2,1)S(1)}, bf16[8,32,256]{2,1,0:T(8,128)(2,1)S(1)}, u32[]{:S(2)}, u32[]{:S(2)}) collective-permute-start(bf16[8,32,256]{2,1,0:T(8,128)(2,1)S(1)} %slice_bitcast_fusion.1), channel_id=1, source_target_pairs={{0,4},{1,5},{2,6},{3,7},{4,0},{5,1},{6,2},{7,3},{8,12},{9,13},{10,... | collective-permute-start | bytes 393224 | tf_op jit(solution)/shard_map/ppermute | solution.py:155
  6.7 0.7 %collective-permute-start.5 = (bf16[8,32,256]{2,1,0:T(8,128)(2,1)S(1)}, bf16[8,32,256]{2,1,0:T(8,128)(2,1)S(1)}, u32[]{:S(2)}, u32[]{:S(2)}) collective-permute-start(bf16[8,32,256]{2,1,0:T(8,128)(2,1)S(1)} %slice_bitcast_fusion.1), channel_id=1, source_target_pairs={{2,4},{3,5},{4,2},{5,3},{10,12},{11,13},{12,10},{13,11},{18,20},{1... | collective-permute-start | bytes 393224 | tf_op jit(solution)/shard_map/ppermute | solution.py:156
  7.3 1.0 %slice_bitcast_fusion = bf16[8,32,256]{2,1,0:T(8,128)(2,1)S(1)} fusion(bf16[2,8,32,256]{3,2,1,0:T(8,128)(2,1)} %refs_0_.3), kind=kLoop, calls=%fused_computation | loop fusion | bytes 262144 | tf_op jit(solution)/shard_map/squeeze | solution.py:151
  8.3 3.2 %collective-permute-start.12 = (bf16[8,32,256]{2,1,0:T(8,128)(2,1)S(1)}, bf16[8,32,256]{2,1,0:T(8,128)(2,1)S(1)}, u32[]{:S(2)}, u32[]{:S(2)}) collective-permute-start(bf16[8,32,256]{2,1,0:T(8,128)(2,1)S(1)} %slice_bitcast_fusion), channel_id=1, source_target_pairs={{7,3},{6,2},{5,1},{4,0},{3,7},{2,6},{1,5},{0,4},{15,11},{14,10},{1... | collective-permute-start | bytes 393224 | tf_op jit(solution)/shard_map/ppermute | solution.py:155
  11.5 0.7 %collective-permute-start.14 = (bf16[8,32,256]{2,1,0:T(8,128)(2,1)S(1)}, bf16[8,32,256]{2,1,0:T(8,128)(2,1)S(1)}, u32[]{:S(2)}, u32[]{:S(2)}) collective-permute-start(bf16[8,32,256]{2,1,0:T(8,128)(2,1)S(1)} %slice_bitcast_fusion), channel_id=1, source_target_pairs={{5,3},{4,2},{3,5},{2,4},{13,11},{12,10},{11,13},{10,12},{21,19},{2... | collective-permute-start | bytes 393224 | tf_op jit(solution)/shard_map/ppermute | solution.py:156
  12.7 1.3 %collective-permute-start.7 = (bf16[8,32,256]{2,1,0:T(8,128)(2,1)S(1)}, bf16[8,32,256]{2,1,0:T(8,128)(2,1)S(1)}, u32[]{:S(2)}, u32[]{:S(2)}) collective-permute-start(bf16[8,32,256]{2,1,0:T(8,128)(2,1)S(1)} %collective-permute-done.3.refs_4_), channel_id=1, source_target_pairs={{2,0},{3,1},{4,6},{5,7},{10,8},{11,9},{12,14},{13,15},{18,16},{19,... | collective-permute-start | bytes 393224 | tf_op jit(solution)/shard_map/ppermute | solution.py:164
  14.0 8.6 %collective-permute-done.12.refs_4_ = bf16[8,32,256]{2,1,0:T(8,128)(2,1)S(1)} collective-permute-done((bf16[8,32,256]{2,1,0:T(8,128)(2,1)S(1)}, bf16[8,32,256]{2,1,0:T(8,128)(2,1)S(1)}, u32[]{:S(2)}, u32[]{:S(2)}) %collective-permute-start.12) | collective-permute-done | bytes 131104 | tf_op jit(solution)/shard_map/ppermute | solution.py:155
  23.1 0.7 %collective-permute-start.6 = (bf16[8,32,256]{2,1,0:T(8,128)(2,1)S(1)}, bf16[8,32,256]{2,1,0:T(8,128)(2,1)S(1)}, u32[]{:S(2)}, u32[]{:S(2)}) collective-permute-start(bf16[8,32,256]{2,1,0:T(8,128)(2,1)S(1)} %collective-permute-done.5.refs_6_), channel_id=1, source_target_pairs={{2,3},{3,2},{4,5},{5,4},{10,11},{11,10},{12,13},{13,12},{18,19},{1... | collective-permute-start | bytes 393224 | tf_op jit(solution)/shard_map/ppermute | solution.py:167
  23.7 0.8 %collective-permute-done.7.refs_8_ = bf16[8,32,256]{2,1,0:T(8,128)(2,1)S(1)} collective-permute-done((bf16[8,32,256]{2,1,0:T(8,128)(2,1)S(1)}, bf16[8,32,256]{2,1,0:T(8,128)(2,1)S(1)}, u32[]{:S(2)}, u32[]{:S(2)}) %collective-permute-start.7) | collective-permute-done | bytes 131104 | tf_op jit(solution)/shard_map/ppermute | solution.py:164
  24.5 1.3 %collective-permute-start.16 = (bf16[8,32,256]{2,1,0:T(8,128)(2,1)S(1)}, bf16[8,32,256]{2,1,0:T(8,128)(2,1)S(1)}, u32[]{:S(2)}, u32[]{:S(2)}) collective-permute-start(bf16[8,32,256]{2,1,0:T(8,128)(2,1)S(1)} %collective-permute-done.12.refs_4_), channel_id=1, source_target_pairs={{5,7},{4,6},{3,1},{2,0},{13,15},{12,14},{11,9},{10,8},{21,23},{20,... | collective-permute-start | bytes 393224 | tf_op jit(solution)/shard_map/ppermute | solution.py:164
  25.8 1.9 %collective-permute-start.8 = (bf16[8,32,256]{2,1,0:T(8,128)(2,1)S(1)}, bf16[8,32,256]{2,1,0:T(8,128)(2,1)S(1)}, u32[]{:S(2)}, u32[]{:S(2)}) collective-permute-start(bf16[8,32,256]{2,1,0:T(8,128)(2,1)S(1)} %collective-permute-done.7.refs_8_), channel_id=1, source_target_pairs={{0,1},{1,0},{6,7},{7,6},{8,9},{9,8},{14,15},{15,14},{16,17},{17,16... | collective-permute-start | bytes 393224 | tf_op jit(solution)/shard_map/ppermute | solution.py:168
  27.7 1.9 %copy-done = bf16[4,6,256,256]{3,2,1,0:T(8,128)(2,1)S(1)} copy-done((bf16[4,6,256,256]{3,2,1,0:T(8,128)(2,1)S(1)}, bf16[4,6,256,256]{3,2,1,0:T(8,128)(2,1)}, u32[]{:S(2)}) %copy-start) | copy-done | bytes 3145752
  30.5 0.7 %collective-permute-start.15 = (bf16[8,32,256]{2,1,0:T(8,128)(2,1)S(1)}, bf16[8,32,256]{2,1,0:T(8,128)(2,1)S(1)}, u32[]{:S(2)}, u32[]{:S(2)}) collective-permute-start(bf16[8,32,256]{2,1,0:T(8,128)(2,1)S(1)} %collective-permute-done.14.refs_6_), channel_id=1, source_target_pairs={{5,4},{4,5},{3,2},{2,3},{13,12},{12,13},{11,10},{10,11},{21,20},{2... | collective-permute-start | bytes 393224 | tf_op jit(solution)/shard_map/ppermute | solution.py:167
  31.1 1.1 %collective-permute-done.16.refs_8_ = bf16[8,32,256]{2,1,0:T(8,128)(2,1)S(1)} collective-permute-done((bf16[8,32,256]{2,1,0:T(8,128)(2,1)S(1)}, bf16[8,32,256]{2,1,0:T(8,128)(2,1)S(1)}, u32[]{:S(2)}, u32[]{:S(2)}) %collective-permute-start.16) | collective-permute-done | bytes 131104 | tf_op jit(solution)/shard_map/ppermute | solution.py:164
  32.3 1.9 %collective-permute-start.17 = (bf16[8,32,256]{2,1,0:T(8,128)(2,1)S(1)}, bf16[8,32,256]{2,1,0:T(8,128)(2,1)S(1)}, u32[]{:S(2)}, u32[]{:S(2)}) collective-permute-start(bf16[8,32,256]{2,1,0:T(8,128)(2,1)S(1)} %collective-permute-done.16.refs_8_), channel_id=1, source_target_pairs={{7,6},{6,7},{1,0},{0,1},{15,14},{14,15},{9,8},{8,9},{23,22},{22,23... | collective-permute-start | bytes 393224 | tf_op jit(solution)/shard_map/ppermute | solution.py:168
  34.2 1.8 %product.2 = (f32[4,64,256]{2,1,0:T(8,128)S(1)}, s16[272,256]{1,0:T(8,128)(2,1)S(1)}, s16[272,256]{1,0:T(8,128)(2,1)S(1)}, s16[272,256]{1,0:T(8,128)(2,1)S(1)}) custom-call(s32[4,6]{1,0:T(4,128)S(1)} %copy-done.2, s32[4]{0:T(128)S(1)} %bitcast.5, bf16[2,8,32,256]{3,2,1,0:T(8,128)(2,1)S(1)} %copy-done.1, ...), custom_call_target="tpu_custom_call" | custom-call | flops 805306368 | bytes 3145728 | tf_op jit(solution)/shard_map/product/pallas_call | solution.py:205
  36.0 1.6 %collective-permute-start.10 = (s16[272,256]{1,0:T(8,128)(2,1)S(1)}, s16[272,256]{1,0:T(8,128)(2,1)S(1)}, u32[]{:S(2)}, u32[]{:S(2)}) collective-permute-start(s16[272,256]{1,0:T(8,128)(2,1)S(1)} %get-tuple-element.18), channel_id=1, source_target_pairs={{0,16},{8,24},{16,0},{24,8},{1,17},{9,25},{17,1},{25,9},{2,18},{10... | collective-permute-start | bytes 417800 | tf_op jit(solution)/shard_map/ppermute | solution.py:121
  37.6 1.4 %collective-permute-start.11 = (s16[272,256]{1,0:T(8,128)(2,1)S(1)}, s16[272,256]{1,0:T(8,128)(2,1)S(1)}, u32[]{:S(2)}, u32[]{:S(2)}) collective-permute-start(s16[272,256]{1,0:T(8,128)(2,1)S(1)} %get-tuple-element.19), channel_id=1, source_target_pairs={{0,24},{8,16},{16,8},{24,0},{1,25},{9,17},{17,9},{25,1},{2,26},{10... | collective-permute-start | bytes 417800 | tf_op jit(solution)/shard_map/ppermute | solution.py:121
  39.6 1.8 %product.3 = (f32[4,64,256]{2,1,0:T(8,128)S(1)}, s16[272,256]{1,0:T(8,128)(2,1)S(1)}, s16[272,256]{1,0:T(8,128)(2,1)S(1)}, s16[272,256]{1,0:T(8,128)(2,1)S(1)}) custom-call(s32[4,6]{1,0:T(4,128)S(1)} %copy-done.2, s32[4]{0:T(128)S(1)} %bitcast.6, bf16[2,8,32,256]{3,2,1,0:T(8,128)(2,1)S(1)} %copy-done.1, ...), custom_call_target="tpu_custom_call" | custom-call | flops 805306368 | bytes 3145728 | tf_op jit(solution)/shard_map/product/pallas_call | solution.py:205
  41.4 1.6 %collective-permute-start.18 = (s16[272,256]{1,0:T(8,128)(2,1)S(1)}, s16[272,256]{1,0:T(8,128)(2,1)S(1)}, u32[]{:S(2)}, u32[]{:S(2)}) collective-permute-start(s16[272,256]{1,0:T(8,128)(2,1)S(1)} %get-tuple-element.22), channel_id=1, source_target_pairs={{24,16},{16,24},{8,0},{0,8},{25,17},{17,25},{9,1},{1,9},{26,18},{1... | collective-permute-start | bytes 417800 | tf_op jit(solution)/shard_map/ppermute | solution.py:121
  43.0 1.5 %collective-permute-start.19 = (s16[272,256]{1,0:T(8,128)(2,1)S(1)}, s16[272,256]{1,0:T(8,128)(2,1)S(1)}, u32[]{:S(2)}, u32[]{:S(2)}) collective-permute-start(s16[272,256]{1,0:T(8,128)(2,1)S(1)} %get-tuple-element.23), channel_id=1, source_target_pairs={{24,8},{16,0},{8,24},{0,16},{25,9},{17,1},{9,25},{1,17},{26,10},{1... | collective-permute-start | bytes 417800 | tf_op jit(solution)/shard_map/ppermute | solution.py:121
  44.5 0.8 %collective-permute-done.10.refs_1_ = s16[272,256]{1,0:T(8,128)(2,1)S(1)} collective-permute-done((s16[272,256]{1,0:T(8,128)(2,1)S(1)}, s16[272,256]{1,0:T(8,128)(2,1)S(1)}, u32[]{:S(2)}, u32[]{:S(2)}) %collective-permute-start.10) | collective-permute-done | bytes 139296 | tf_op jit(solution)/shard_map/ppermute | solution.py:121
  45.3 2.8 %collective-permute-start.20 = (s16[272,256]{1,0:T(8,128)(2,1)S(1)}, s16[272,256]{1,0:T(8,128)(2,1)S(1)}, u32[]{:S(2)}, u32[]{:S(2)}) collective-permute-start(s16[272,256]{1,0:T(8,128)(2,1)S(1)} %get-tuple-element.24), channel_id=1, source_target_pairs={{24,0},{16,8},{8,16},{0,24},{25,1},{17,9},{9,17},{1,25},{26,2},{18... | collective-permute-start | bytes 417800 | tf_op jit(solution)/shard_map/ppermute | solution.py:121
  48.3 1.9 %collective-permute-done.18.refs_0_ = s16[272,256]{1,0:T(8,128)(2,1)S(1)} collective-permute-done((s16[272,256]{1,0:T(8,128)(2,1)S(1)}, s16[272,256]{1,0:T(8,128)(2,1)S(1)}, u32[]{:S(2)}, u32[]{:S(2)}) %collective-permute-start.18) | collective-permute-done | bytes 139296 | tf_op jit(solution)/shard_map/ppermute | solution.py:121
  50.1 3.2 %collective-permute-done.20.refs_2_ = s16[272,256]{1,0:T(8,128)(2,1)S(1)} collective-permute-done((s16[272,256]{1,0:T(8,128)(2,1)S(1)}, s16[272,256]{1,0:T(8,128)(2,1)S(1)}, u32[]{:S(2)}, u32[]{:S(2)}) %collective-permute-start.20) | collective-permute-done | bytes 139296 | tf_op jit(solution)/shard_map/ppermute | solution.py:121
  53.5 1.6 %collective-permute-start.21 = (f32[4,256]{1,0:T(4,128)S(1)}, f32[4,256]{1,0:T(4,128)S(1)}, u32[]{:S(2)}, u32[]{:S(2)}) collective-permute-start(f32[4,256]{1,0:T(4,128)S(1)} %get-tuple-element.28.refs_2_), channel_id=1, source_target_pairs={{0,8},{8,0},{16,24},{24,16},{1,9},{9,1},{17,25},{25,17},{2,10},{10... | collective-permute-start | bytes 12296 | tf_op jit(solution)/shard_map/ppermute | solution.py:121
  55.6 1.5 %collective-permute-start.23 = (f32[4,256]{1,0:T(4,128)S(1)}, f32[4,256]{1,0:T(4,128)S(1)}, u32[]{:S(2)}, u32[]{:S(2)}) collective-permute-start(f32[4,256]{1,0:T(4,128)S(1)} %get-tuple-element.28.refs_2_), channel_id=1, source_target_pairs={{0,24},{8,16},{16,8},{24,0},{1,25},{9,17},{17,9},{25,1},{2,26},{10... | collective-permute-start | bytes 12296 | tf_op jit(solution)/shard_map/ppermute | solution.py:121
  57.2 1.5 %collective-permute-done.22.refs_4_ = f32[4,256]{1,0:T(4,128)S(1)} collective-permute-done((f32[4,256]{1,0:T(4,128)S(1)}, f32[4,256]{1,0:T(4,128)S(1)}, u32[]{:S(2)}, u32[]{:S(2)}) %collective-permute-start.22) | collective-permute-done | bytes 4128 | tf_op jit(solution)/shard_map/ppermute | solution.py:121
  58.7 1.4 %collective-permute-done.23.refs_5_ = f32[4,256]{1,0:T(4,128)S(1)} collective-permute-done((f32[4,256]{1,0:T(4,128)S(1)}, f32[4,256]{1,0:T(4,128)S(1)}, u32[]{:S(2)}, u32[]{:S(2)}) %collective-permute-start.23) | collective-permute-done | bytes 4128 | tf_op jit(solution)/shard_map/ppermute | solution.py:121
  60.1 0.7 %scale.1 = bf16[2,4,64,256]{3,2,1,0:T(8,128)(2,1)} custom-call(f32[4,64,256]{2,1,0:T(8,128)S(1)} %get-tuple-element.21.refs_0_, f32[4,64,256]{2,1,0:T(8,128)S(1)} %get-tuple-element.27.refs_1_, f32[4,256]{1,0:T(4,128)S(1)} %get-tuple-element.28.refs_2_, f32[4,256]{1,0:T(4,128)S(1)} %collective-permute-done.21.refs_3_, ...), custom_call_target="tpu_custom_call" | custom-call | tf_op jit(solution)/shard_map/scale/pallas_call | solution.py:224
  (32 shorter events, 3.4 us)
Async XLA Ops:
  0.0 22.5 %collective-permute-start.1 = (bf16[2,8,32,256]{3,2,1,0:T(8,128)(2,1)}, bf16[2,8,32,256]{3,2,1,0:T(8,128)(2,1)S(1)}, u32[]{:S(2)}, u32[]{:S(2)}) collective-permute-start(bf16[2,8,32,256]{3,2,1,0:T(8,128)(2,1)} %refs_0_.3), channel_id=1, source_target_pairs={{0,2},{1,3},{2,0},{3,1},{4,6},{5,7},{6,4},{7,5},{8,10},{9,11},{10,... | collective-permute-start | bytes 786440 | tf_op jit(solution)/shard_map/ppermute | solution.py:157
  3.1 31.1 %copy-start.2 = (s32[4,6]{1,0:T(4,128)S(1)}, s32[4,6]{1,0:T(4,128)}, u32[]{:S(2)}) copy-start(s32[4,6]{1,0:T(4,128)} %index_ref.3) | copy-start | bytes 292
  3.1 31.2 %copy-start.3 = (s32[4,1]{0,1:T(1,128)S(1)}, s32[4,1]{0,1:T(1,128)}, u32[]{:S(2)}) copy-start(s32[4,1]{0,1:T(1,128)} %param.7) | copy-start | bytes 52
  4.0 8.7 %collective-permute-start.3 = (bf16[8,32,256]{2,1,0:T(8,128)(2,1)S(1)}, bf16[8,32,256]{2,1,0:T(8,128)(2,1)S(1)}, u32[]{:S(2)}, u32[]{:S(2)}) collective-permute-start(bf16[8,32,256]{2,1,0:T(8,128)(2,1)S(1)} %slice_bitcast_fusion.1), channel_id=1, source_target_pairs={{0,4},{1,5},{2,6},{3,7},{4,0},{5,1},{6,2},{7,3},{8,12},{9,13},{10,... | collective-permute-start | bytes 393224 | tf_op jit(solution)/shard_map/ppermute | solution.py:155
  6.7 6.0 %collective-permute-start.5 = (bf16[8,32,256]{2,1,0:T(8,128)(2,1)S(1)}, bf16[8,32,256]{2,1,0:T(8,128)(2,1)S(1)}, u32[]{:S(2)}, u32[]{:S(2)}) collective-permute-start(bf16[8,32,256]{2,1,0:T(8,128)(2,1)S(1)} %slice_bitcast_fusion.1), channel_id=1, source_target_pairs={{2,4},{3,5},{4,2},{5,3},{10,12},{11,13},{12,10},{13,11},{18,20},{1... | collective-permute-start | bytes 393224 | tf_op jit(solution)/shard_map/ppermute | solution.py:156
  7.3 26.9 %copy-start.1 = (bf16[2,8,32,256]{3,2,1,0:T(8,128)(2,1)S(1)}, bf16[2,8,32,256]{3,2,1,0:T(8,128)(2,1)}, u32[]{:S(2)}) copy-start(bf16[2,8,32,256]{3,2,1,0:T(8,128)(2,1)} %refs_0_.3) | copy-start | bytes 786436
  8.3 14.2 %collective-permute-start.12 = (bf16[8,32,256]{2,1,0:T(8,128)(2,1)S(1)}, bf16[8,32,256]{2,1,0:T(8,128)(2,1)S(1)}, u32[]{:S(2)}, u32[]{:S(2)}) collective-permute-start(bf16[8,32,256]{2,1,0:T(8,128)(2,1)S(1)} %slice_bitcast_fusion), channel_id=1, source_target_pairs={{7,3},{6,2},{5,1},{4,0},{3,7},{2,6},{1,5},{0,4},{15,11},{14,10},{1... | collective-permute-start | bytes 393224 | tf_op jit(solution)/shard_map/ppermute | solution.py:155
  11.5 11.5 %collective-permute-start.14 = (bf16[8,32,256]{2,1,0:T(8,128)(2,1)S(1)}, bf16[8,32,256]{2,1,0:T(8,128)(2,1)S(1)}, u32[]{:S(2)}, u32[]{:S(2)}) collective-permute-start(bf16[8,32,256]{2,1,0:T(8,128)(2,1)S(1)} %slice_bitcast_fusion), channel_id=1, source_target_pairs={{5,3},{4,2},{3,5},{2,4},{13,11},{12,10},{11,13},{10,12},{21,19},{2... | collective-permute-start | bytes 393224 | tf_op jit(solution)/shard_map/ppermute | solution.py:156
  12.7 17.8 %collective-permute-start = (bf16[2,8,32,256]{3,2,1,0:T(8,128)(2,1)}, bf16[2,8,32,256]{3,2,1,0:T(8,128)(2,1)S(1)}, u32[]{:S(2)}, u32[]{:S(2)}) collective-permute-start(bf16[2,8,32,256]{3,2,1,0:T(8,128)(2,1)} %refs_0_.3), channel_id=1, source_target_pairs={{0,1},{1,0},{2,3},{3,2},{4,5},{5,4},{6,7},{7,6},{8,9},{9,8},{10,11... | collective-permute-start | bytes 786440 | tf_op jit(solution)/shard_map/ppermute | solution.py:158
  12.7 11.8 %collective-permute-start.7 = (bf16[8,32,256]{2,1,0:T(8,128)(2,1)S(1)}, bf16[8,32,256]{2,1,0:T(8,128)(2,1)S(1)}, u32[]{:S(2)}, u32[]{:S(2)}) collective-permute-start(bf16[8,32,256]{2,1,0:T(8,128)(2,1)S(1)} %collective-permute-done.3.refs_4_), channel_id=1, source_target_pairs={{2,0},{3,1},{4,6},{5,7},{10,8},{11,9},{12,14},{13,15},{18,16},{19,... | collective-permute-start | bytes 393224 | tf_op jit(solution)/shard_map/ppermute | solution.py:164
  22.5 3.3 %collective-permute-start.4 = (bf16[8,32,256]{2,1,0:T(8,128)(2,1)S(1)}, bf16[8,32,256]{2,1,0:T(8,128)(2,1)S(1)}, u32[]{:S(2)}, u32[]{:S(2)}) collective-permute-start(bf16[8,32,256]{2,1,0:T(8,128)(2,1)S(1)} %collective-permute-done.3.refs_4_), channel_id=1, source_target_pairs={{0,1},{1,0},{2,3},{3,2},{4,5},{5,4},{6,7},{7,6},{8,9},{9,8},{10,11... | collective-permute-start | bytes 393224 | tf_op jit(solution)/shard_map/ppermute | solution.py:166
  22.6 11.6 %collective-permute-start.2 = (bf16[2,8,32,256]{3,2,1,0:T(8,128)(2,1)S(1)}, bf16[2,8,32,256]{3,2,1,0:T(8,128)(2,1)S(1)}, u32[]{:S(2)}, u32[]{:S(2)}) collective-permute-start(bf16[2,8,32,256]{3,2,1,0:T(8,128)(2,1)S(1)} %collective-permute-done.1.refs_2_), channel_id=1, source_target_pairs={{7,6},{6,7},{5,4},{4,5},{3,2},{2,3},{1,0},{0,1},{15,14},{14,15},{1... | collective-permute-start | bytes 786440 | tf_op jit(solution)/shard_map/ppermute | solution.py:159
  23.1 6.8 %collective-permute-start.6 = (bf16[8,32,256]{2,1,0:T(8,128)(2,1)S(1)}, bf16[8,32,256]{2,1,0:T(8,128)(2,1)S(1)}, u32[]{:S(2)}, u32[]{:S(2)}) collective-permute-start(bf16[8,32,256]{2,1,0:T(8,128)(2,1)S(1)} %collective-permute-done.5.refs_6_), channel_id=1, source_target_pairs={{2,3},{3,2},{4,5},{5,4},{10,11},{11,10},{12,13},{13,12},{18,19},{1... | collective-permute-start | bytes 393224 | tf_op jit(solution)/shard_map/ppermute | solution.py:167
  24.5 7.8 %collective-permute-start.16 = (bf16[8,32,256]{2,1,0:T(8,128)(2,1)S(1)}, bf16[8,32,256]{2,1,0:T(8,128)(2,1)S(1)}, u32[]{:S(2)}, u32[]{:S(2)}) collective-permute-start(bf16[8,32,256]{2,1,0:T(8,128)(2,1)S(1)} %collective-permute-done.12.refs_4_), channel_id=1, source_target_pairs={{5,7},{4,6},{3,1},{2,0},{13,15},{12,14},{11,9},{10,8},{21,23},{20,... | collective-permute-start | bytes 393224 | tf_op jit(solution)/shard_map/ppermute | solution.py:164
  25.8 8.4 %collective-permute-start.8 = (bf16[8,32,256]{2,1,0:T(8,128)(2,1)S(1)}, bf16[8,32,256]{2,1,0:T(8,128)(2,1)S(1)}, u32[]{:S(2)}, u32[]{:S(2)}) collective-permute-start(bf16[8,32,256]{2,1,0:T(8,128)(2,1)S(1)} %collective-permute-done.7.refs_8_), channel_id=1, source_target_pairs={{0,1},{1,0},{6,7},{7,6},{8,9},{9,8},{14,15},{15,14},{16,17},{17,16... | collective-permute-start | bytes 393224 | tf_op jit(solution)/shard_map/ppermute | solution.py:168
  27.7 1.9 %copy-start = (bf16[4,6,256,256]{3,2,1,0:T(8,128)(2,1)S(1)}, bf16[4,6,256,256]{3,2,1,0:T(8,128)(2,1)}, u32[]{:S(2)}) copy-start(bf16[4,6,256,256]{3,2,1,0:T(8,128)(2,1)} %right_ref.1) | copy-start | bytes 9437188
  29.9 9.2 %collective-permute-start.13 = (bf16[8,32,256]{2,1,0:T(8,128)(2,1)S(1)}, bf16[8,32,256]{2,1,0:T(8,128)(2,1)S(1)}, u32[]{:S(2)}, u32[]{:S(2)}) collective-permute-start(bf16[8,32,256]{2,1,0:T(8,128)(2,1)S(1)} %collective-permute-done.12.refs_4_), channel_id=1, source_target_pairs={{7,6},{6,7},{5,4},{4,5},{3,2},{2,3},{1,0},{0,1},{15,14},{14,15},{1... | collective-permute-start | bytes 393224 | tf_op jit(solution)/shard_map/ppermute | solution.py:166
  30.5 9.1 %collective-permute-start.15 = (bf16[8,32,256]{2,1,0:T(8,128)(2,1)S(1)}, bf16[8,32,256]{2,1,0:T(8,128)(2,1)S(1)}, u32[]{:S(2)}, u32[]{:S(2)}) collective-permute-start(bf16[8,32,256]{2,1,0:T(8,128)(2,1)S(1)} %collective-permute-done.14.refs_6_), channel_id=1, source_target_pairs={{5,4},{4,5},{3,2},{2,3},{13,12},{12,13},{11,10},{10,11},{21,20},{2... | collective-permute-start | bytes 393224 | tf_op jit(solution)/shard_map/ppermute | solution.py:167
  32.3 7.3 %collective-permute-start.17 = (bf16[8,32,256]{2,1,0:T(8,128)(2,1)S(1)}, bf16[8,32,256]{2,1,0:T(8,128)(2,1)S(1)}, u32[]{:S(2)}, u32[]{:S(2)}) collective-permute-start(bf16[8,32,256]{2,1,0:T(8,128)(2,1)S(1)} %collective-permute-done.16.refs_8_), channel_id=1, source_target_pairs={{7,6},{6,7},{1,0},{0,1},{15,14},{14,15},{9,8},{8,9},{23,22},{22,23... | collective-permute-start | bytes 393224 | tf_op jit(solution)/shard_map/ppermute | solution.py:168
  36.0 9.3 %collective-permute-start.10 = (s16[272,256]{1,0:T(8,128)(2,1)S(1)}, s16[272,256]{1,0:T(8,128)(2,1)S(1)}, u32[]{:S(2)}, u32[]{:S(2)}) collective-permute-start(s16[272,256]{1,0:T(8,128)(2,1)S(1)} %get-tuple-element.18), channel_id=1, source_target_pairs={{0,16},{8,24},{16,0},{24,8},{1,17},{9,25},{17,1},{25,9},{2,18},{10... | collective-permute-start | bytes 417800 | tf_op jit(solution)/shard_map/ppermute | solution.py:121
  37.6 10.5 %collective-permute-start.11 = (s16[272,256]{1,0:T(8,128)(2,1)S(1)}, s16[272,256]{1,0:T(8,128)(2,1)S(1)}, u32[]{:S(2)}, u32[]{:S(2)}) collective-permute-start(s16[272,256]{1,0:T(8,128)(2,1)S(1)} %get-tuple-element.19), channel_id=1, source_target_pairs={{0,24},{8,16},{16,8},{24,0},{1,25},{9,17},{17,9},{25,1},{2,26},{10... | collective-permute-start | bytes 417800 | tf_op jit(solution)/shard_map/ppermute | solution.py:121
  39.1 9.0 %collective-permute-start.9 = (s16[272,256]{1,0:T(8,128)(2,1)S(1)}, s16[272,256]{1,0:T(8,128)(2,1)S(1)}, u32[]{:S(2)}, u32[]{:S(2)}) collective-permute-start(s16[272,256]{1,0:T(8,128)(2,1)S(1)} %get-tuple-element.17), channel_id=1, source_target_pairs={{0,8},{8,0},{16,24},{24,16},{1,9},{9,1},{17,25},{25,17},{2,10},{10... | collective-permute-start | bytes 417800 | tf_op jit(solution)/shard_map/ppermute | solution.py:121
  41.4 8.7 %collective-permute-start.18 = (s16[272,256]{1,0:T(8,128)(2,1)S(1)}, s16[272,256]{1,0:T(8,128)(2,1)S(1)}, u32[]{:S(2)}, u32[]{:S(2)}) collective-permute-start(s16[272,256]{1,0:T(8,128)(2,1)S(1)} %get-tuple-element.22), channel_id=1, source_target_pairs={{24,16},{16,24},{8,0},{0,8},{25,17},{17,25},{9,1},{1,9},{26,18},{1... | collective-permute-start | bytes 417800 | tf_op jit(solution)/shard_map/ppermute | solution.py:121
  43.0 7.2 %collective-permute-start.19 = (s16[272,256]{1,0:T(8,128)(2,1)S(1)}, s16[272,256]{1,0:T(8,128)(2,1)S(1)}, u32[]{:S(2)}, u32[]{:S(2)}) collective-permute-start(s16[272,256]{1,0:T(8,128)(2,1)S(1)} %get-tuple-element.23), channel_id=1, source_target_pairs={{24,8},{16,0},{8,24},{0,16},{25,9},{17,1},{9,25},{1,17},{26,10},{1... | collective-permute-start | bytes 417800 | tf_op jit(solution)/shard_map/ppermute | solution.py:121
  45.3 8.0 %collective-permute-start.20 = (s16[272,256]{1,0:T(8,128)(2,1)S(1)}, s16[272,256]{1,0:T(8,128)(2,1)S(1)}, u32[]{:S(2)}, u32[]{:S(2)}) collective-permute-start(s16[272,256]{1,0:T(8,128)(2,1)S(1)} %get-tuple-element.24), channel_id=1, source_target_pairs={{24,0},{16,8},{8,16},{0,24},{25,1},{17,9},{9,17},{1,25},{26,2},{18... | collective-permute-start | bytes 417800 | tf_op jit(solution)/shard_map/ppermute | solution.py:121
  53.5 3.7 %collective-permute-start.21 = (f32[4,256]{1,0:T(4,128)S(1)}, f32[4,256]{1,0:T(4,128)S(1)}, u32[]{:S(2)}, u32[]{:S(2)}) collective-permute-start(f32[4,256]{1,0:T(4,128)S(1)} %get-tuple-element.28.refs_2_), channel_id=1, source_target_pairs={{0,8},{8,0},{16,24},{24,16},{1,9},{9,1},{17,25},{25,17},{2,10},{10... | collective-permute-start | bytes 12296 | tf_op jit(solution)/shard_map/ppermute | solution.py:121
  55.1 3.6 %collective-permute-start.22 = (f32[4,256]{1,0:T(4,128)S(1)}, f32[4,256]{1,0:T(4,128)S(1)}, u32[]{:S(2)}, u32[]{:S(2)}) collective-permute-start(f32[4,256]{1,0:T(4,128)S(1)} %get-tuple-element.28.refs_2_), channel_id=1, source_target_pairs={{0,16},{8,24},{16,0},{24,8},{1,17},{9,25},{17,1},{25,9},{2,18},{10... | collective-permute-start | bytes 12296 | tf_op jit(solution)/shard_map/ppermute | solution.py:121
  55.6 4.5 %collective-permute-start.23 = (f32[4,256]{1,0:T(4,128)S(1)}, f32[4,256]{1,0:T(4,128)S(1)}, u32[]{:S(2)}, u32[]{:S(2)}) collective-permute-start(f32[4,256]{1,0:T(4,128)S(1)} %get-tuple-element.28.refs_2_), channel_id=1, source_target_pairs={{0,24},{8,16},{16,8},{24,0},{1,25},{9,17},{17,9},{25,1},{2,26},{10... | collective-permute-start | bytes 12296 | tf_op jit(solution)/shard_map/ppermute | solution.py:121

commit v2 on v0

--- a/solution.py
+++ b/solution.py
@@ -11,7 +11,7 @@
 OFFSET = 32640
 LOG_STEPS = 256.0
 CODE_ROWS = 16
-MAX_DIRECT = 8
+LINE = 4
 
 VMEM = pl.BlockSpec(memory_space=pltpu.VMEM)
 SMEM = pl.BlockSpec(memory_space=pltpu.SMEM)
@@ -28,8 +28,16 @@
         copy.wait()
 
 
-def product_kernel(n_row, shifts, index_ref, count_ref, *refs):
-    n_block = len(shifts)
+def join_kernel(mine_ref, other_ref, *out_refs):
+    rows = mine_ref.shape[2]
+    core = lax.axis_index("col") & 1
+    for a, out_ref in enumerate(out_refs):
+        out_ref[:, pl.ds(pl.multiple_of(core * rows, rows), rows), :] = mine_ref[a]
+        out_ref[:, pl.ds(pl.multiple_of((1 - core) * rows, rows), rows), :] = other_ref[a]
+
+
+def product_kernel(n_row, steps, index_ref, count_ref, *refs):
+    n_block = len(steps)
     blocks, right_ref = refs[:n_block], refs[n_block]
     own_ref = refs[n_block + 1]
     sent_refs = refs[n_block + 2 : n_block + 1 + n_row]
@@ -38,13 +46,21 @@
     kept = left.shape[0] - 1
     part = tile // n_row
     row = lax.axis_index("row")
-    for block, shift in zip(blocks, shifts):
+    for block, step in zip(blocks, steps):
         rows = block.shape[1]
-        if n_block == 1:
+        if rows == tile:
             left[:kept] = block[...]
+            continue
+        col = lax.axis_index("col")
+        source = (col >> 1) + (2 * (col & 1) - 1) * step
+
+        def place(block=block, source=source, rows=rows):
+            left[:kept, pl.ds(pl.multiple_of(source * rows, rows), rows), :] = block[...]
+
+        if step:
+            pl.when((source >= 0) & (source < tile // rows))(place)
         else:
-            start = pl.multiple_of((lax.axis_index("col") ^ shift) * rows, rows)
-            left[:kept, pl.ds(start, rows), :] = block[...]
+            place()
     left[kept] = jnp.zeros(left.shape[1:], left.dtype)
     lines = lax.broadcasted_iota(jnp.int32, (CODE_ROWS, tile), 0)
     codes = jnp.zeros((CODE_ROWS, tile), jnp.int32)
@@ -116,29 +132,48 @@
     return pltpu.CompilerParams(vmem_limit_bytes=mib << 20)
 
 
-def is_direct(n_col):
-    return n_col <= MAX_DIRECT and n_col & (n_col - 1) == 0
+def is_line(n_col):
+    return n_col == 2 * LINE
+
+
+def both_ways(moves):
+    up = [(2 * i, 2 * j) for i, j in moves]
+    return up + [(2 * LINE - 1 - i, 2 * LINE - 1 - j) for i, j in up]
 
 
 def shards(n_row, n_col, left_tiles, right, right_index, right_count):
-    windows, kept, _, tile = left_tiles.shape
+    windows, kept, rows, tile = left_tiles.shape
     column_blocks, slots = right.shape[:2]
     part = tile // n_row
     right_count = right_count.reshape(-1)
 
-    if is_direct(n_col):
-        shifts = tuple(range(n_col))
-        mine = [left_tiles[a] for a in range(windows)]
-        gathered = [[None] * n_col for _ in range(windows)]
+    if is_line(n_col):
+        swap = [(i, i ^ 1) for i in range(n_col)]
+        pair = lax.ppermute(left_tiles, "col", swap)
+        joined = pl.pallas_call(
+            join_kernel,
+            out_shape=[jax.ShapeDtypeStruct((kept, 2 * rows, tile), left_tiles.dtype)] * windows,
+            in_specs=[VMEM] * 2,
+            out_specs=[VMEM] * windows,
+            compiler_params=limits(8),
+            name="join",
+        )(left_tiles, pair)
+        first = both_ways([(i, i + 1) for i in range(LINE - 1)])
+        second = both_ways([(i, i + 1) for i in range(1, LINE - 1)])
+        third = both_ways([(1, LINE - 1)])
+        steps = (0, 1, -1, 2, -2, 3, -3)
+        gathered = []
         for a in range(windows):
-            gathered[a][0] = mine[a]
-            for k in range(2, n_col, 2):
-                gathered[a][k] = exchange(mine[a], "col", n_col, k, flip=a % 2 == 1)
-        for a in range(windows):
-            for k in range(0, n_col, 2):
-                gathered[a][k + 1] = exchange(gathered[a][k], "col", n_col, 1, flip=a % 2 == 1)
+            flip = -1 if a % 2 else 1
+            one = lax.ppermute(joined[a], "col", first[::flip])
+            two = lax.ppermute(one, "col", second[::flip])
+            three = lax.ppermute(one, "col", third[::flip])
+            blocks = [joined[a]]
+            for x in (one, two, three):
+                blocks += [x, lax.ppermute(x, "col", swap[::flip])]
+            gathered.append(blocks)
     else:
-        shifts = (0,)
+        steps = (0,)
         whole = lax.all_gather(left_tiles, "col", axis=2, tiled=True)
         gathered = [[whole[a]] for a in range(windows)]
 
@@ -153,10 +188,10 @@
     )(right)
     sent_rows = column_blocks * part + CODE_ROWS
     multiply = pl.pallas_call(
-        functools.partial(product_kernel, n_row, shifts),
+        functools.partial(product_kernel, n_row, steps),
         out_shape=[jax.ShapeDtypeStruct((column_blocks, part, tile), jnp.float32)]
         + [jax.ShapeDtypeStruct((sent_rows, tile), jnp.int16)] * (n_row - 1),
-        in_specs=[SMEM] * 2 + [VMEM] * (len(shifts) + 1),
+        in_specs=[SMEM] * 2 + [VMEM] * (len(steps) + 1),
         out_specs=[VMEM] * n_row,
         scratch_shapes=[
             pltpu.VMEM((kept + 1, tile, tile), left_tiles.dtype),

time: 54.7 us -> 57.5 us (1.051)
  starting transfers between devices: 24.2 us -> 36.6 us
  waiting for transfers between devices: 22.4 us -> 12.5 us
    ppermute x0 -> x13, starting transfers between devices: none -> 25.9 us  [the longest x6 14.4 us: shards(): blocks += [x, lax.ppermute(x, 'col', swap[::flip])]]
    ppermute x23 -> x9, starting transfers between devices: 24.2 us -> 10.8 us  [exchange(): return lax.ppermute(x, axis, pairs[::-1] if flip else pairs)]
    ppermute x23 -> x9, waiting for transfers between devices: 22.4 us -> 9.65 us  [exchange(): return lax.ppermute(x, axis, pairs[::-1] if flip else pairs)]
    ppermute x0 -> x13, waiting for transfers between devices: none -> 2.87 us  [the longest x2 1.47 us: shards(): one = lax.ppermute(joined[a], 'col', first[::flip])]
    squeeze x1 -> x0, local copies, waits for them, and re-layouts: 0.98 us -> none  [shards(): mine = [left_tiles[a] for a in range(windows)]]
    unnamed x6 -> x8, local copies, waits for them, and re-layouts: 1.9 us -> 2.85 us
  transfers between devices with their start and end apart: 23 -> 22, of which waited for: 10 -> 10; matrix products, arithmetic and copies ran while one was open for 0% -> 0% of each run, Pallas kernels for 7% -> 7%
where the time goes in v2:
time: 57.5 us; the launch traced here: 57.2 us
  starting transfers between devices  36.6 us (64%)
  waiting for transfers between devices  12.5 us (22%)
  Pallas kernels  5.04 us (9%)
  local copies, waits for them, and re-layouts  2.85 us (5%)
    ppermute x6, starting transfers between devices, shards(): blocks += [x, lax.ppermute(x, 'col', swap[::flip])]  14.4 us
    ppermute x9, starting transfers between devices, exchange(): return lax.ppermute(x, axis, pairs[::-1] if flip else pairs)  10.8 us
    ppermute x9, waiting for transfers between devices, exchange(): return lax.ppermute(x, axis, pairs[::-1] if flip else pairs)  9.65 us
    ppermute x2, starting transfers between devices, shards(): one = lax.ppermute(joined[a], 'col', first[::flip])  8.34 us
    pallas_call x2, Pallas kernels, shards(): own, *sent = multiply(right_index, right_count, *gathered[a], staged)  3.65 us
    unnamed x8, local copies, waits for them, and re-layouts  2.85 us
    ppermute x2, waiting for transfers between devices, shards(): one = lax.ppermute(joined[a], 'col', first[::flip])  1.47 us
    ppermute x1, waiting for transfers between devices, shards(): pair = lax.ppermute(left_tiles, 'col', swap)  1.37 us
  transfers between devices with their start and end apart: 22, of which 10 were waited for; matrix products, arithmetic and copies ran while one was open for 0% of the time, Pallas kernels for 7%

profile of v2, /device:TPU:0, one launch (start us, length us, event | category | flops | bytes accessed | tf_op | source)
XLA Modules:
  0.0 57.2 jit_solution(17088203345461678284)
XLA Ops:
  0.5 1.4 %collective-permute-done.other_ref = bf16[2,8,32,256]{3,2,1,0:T(8,128)(2,1)S(1)} collective-permute-done((bf16[2,8,32,256]{3,2,1,0:T(8,128)(2,1)}, bf16[2,8,32,256]{3,2,1,0:T(8,128)(2,1)S(1)}, u32[]{:S(2)}, u32[]{:S(2)}) %collective-permute-start) | collective-permute-done | bytes 262176 | tf_op jit(solution)/shard_map/ppermute | solution.py:152
  1.9 0.9 %copy-done.1 = bf16[2,8,32,256]{3,2,1,0:T(8,128)(2,1)S(1)} copy-done((bf16[2,8,32,256]{3,2,1,0:T(8,128)(2,1)S(1)}, bf16[2,8,32,256]{3,2,1,0:T(8,128)(2,1)}, u32[]{:S(2)}) %copy-start.1) | copy-done | bytes 262168
  2.9 4.9 %collective-permute-start.1 = (bf16[8,64,256]{2,1,0:T(8,128)(2,1)S(1)}, bf16[8,64,256]{2,1,0:T(8,128)(2,1)S(1)}, u32[]{:S(2)}, u32[]{:S(2)}) collective-permute-start(bf16[8,64,256]{2,1,0:T(8,128)(2,1)S(1)} %get-tuple-element.19.refs_0_), channel_id=1, source_target_pairs={{0,2},{2,4},{4,6},{7,5},{5,3},{3,1},{8,10},{10,12},{12,14},{15,13}... | collective-permute-start | bytes 786440 | tf_op jit(solution)/shard_map/ppermute | solution.py:168
  7.7 3.5 %collective-permute-start.10 = (bf16[8,64,256]{2,1,0:T(8,128)(2,1)S(1)}, bf16[8,64,256]{2,1,0:T(8,128)(2,1)S(1)}, u32[]{:S(2)}, u32[]{:S(2)}) collective-permute-start(bf16[8,64,256]{2,1,0:T(8,128)(2,1)S(1)} %get-tuple-element.25.refs_0_), channel_id=1, source_target_pairs={{3,1},{5,3},{7,5},{4,6},{2,4},{0,2},{11,9},{13,11},{15,13},{12,14}... | collective-permute-start | bytes 786440 | tf_op jit(solution)/shard_map/ppermute | solution.py:168
  11.6 0.7 %collective-permute-start.3 = (bf16[8,64,256]{2,1,0:T(8,128)(2,1)S(1)}, bf16[8,64,256]{2,1,0:T(8,128)(2,1)S(1)}, u32[]{:S(2)}, u32[]{:S(2)}) collective-permute-start(bf16[8,64,256]{2,1,0:T(8,128)(2,1)S(1)} %collective-permute-done.1.refs_1_), channel_id=1, source_target_pairs={{2,4},{4,6},{5,3},{3,1},{10,12},{12,14},{13,11},{11,9},{18,20},{20... | collective-permute-start | bytes 786440 | tf_op jit(solution)/shard_map/ppermute | solution.py:169
  12.3 0.7 %collective-permute-start.5 = (bf16[8,64,256]{2,1,0:T(8,128)(2,1)S(1)}, bf16[8,64,256]{2,1,0:T(8,128)(2,1)S(1)}, u32[]{:S(2)}, u32[]{:S(2)}) collective-permute-start(bf16[8,64,256]{2,1,0:T(8,128)(2,1)S(1)} %collective-permute-done.1.refs_1_), channel_id=1, source_target_pairs={{2,6},{5,1},{10,14},{13,9},{18,22},{21,17},{26,30},{29,25}} | collective-permute-start | bytes 786440 | tf_op jit(solution)/shard_map/ppermute | solution.py:170
  13.0 1.0 %collective-permute-start.2 = (bf16[8,64,256]{2,1,0:T(8,128)(2,1)S(1)}, bf16[8,64,256]{2,1,0:T(8,128)(2,1)S(1)}, u32[]{:S(2)}, u32[]{:S(2)}) collective-permute-start(bf16[8,64,256]{2,1,0:T(8,128)(2,1)S(1)} %collective-permute-done.1.refs_1_), channel_id=1, source_target_pairs={{0,1},{1,0},{2,3},{3,2},{4,5},{5,4},{6,7},{7,6},{8,9},{9,8},{10,11... | collective-permute-start | bytes 786440 | tf_op jit(solution)/shard_map/ppermute | solution.py:173
  14.0 1.1 %collective-permute-done.10.refs_1_ = bf16[8,64,256]{2,1,0:T(8,128)(2,1)S(1)} collective-permute-done((bf16[8,64,256]{2,1,0:T(8,128)(2,1)S(1)}, bf16[8,64,256]{2,1,0:T(8,128)(2,1)S(1)}, u32[]{:S(2)}, u32[]{:S(2)}) %collective-permute-start.10) | collective-permute-done | bytes 262176 | tf_op jit(solution)/shard_map/ppermute | solution.py:168
  15.1 0.7 %collective-permute-start.12 = (bf16[8,64,256]{2,1,0:T(8,128)(2,1)S(1)}, bf16[8,64,256]{2,1,0:T(8,128)(2,1)S(1)}, u32[]{:S(2)}, u32[]{:S(2)}) collective-permute-start(bf16[8,64,256]{2,1,0:T(8,128)(2,1)S(1)} %collective-permute-done.10.refs_1_), channel_id=1, source_target_pairs={{3,1},{5,3},{4,6},{2,4},{11,9},{13,11},{12,14},{10,12},{19,17},{21... | collective-permute-start | bytes 786440 | tf_op jit(solution)/shard_map/ppermute | solution.py:169
  15.8 0.7 %collective-permute-start.14 = (bf16[8,64,256]{2,1,0:T(8,128)(2,1)S(1)}, bf16[8,64,256]{2,1,0:T(8,128)(2,1)S(1)}, u32[]{:S(2)}, u32[]{:S(2)}) collective-permute-start(bf16[8,64,256]{2,1,0:T(8,128)(2,1)S(1)} %collective-permute-done.10.refs_1_), channel_id=1, source_target_pairs={{5,1},{2,6},{13,9},{10,14},{21,17},{18,22},{29,25},{26,30}} | collective-permute-start | bytes 786440 | tf_op jit(solution)/shard_map/ppermute | solution.py:170
  16.5 2.3 %collective-permute-start.4 = (bf16[8,64,256]{2,1,0:T(8,128)(2,1)S(1)}, bf16[8,64,256]{2,1,0:T(8,128)(2,1)S(1)}, u32[]{:S(2)}, u32[]{:S(2)}) collective-permute-start(bf16[8,64,256]{2,1,0:T(8,128)(2,1)S(1)} %collective-permute-done.3.refs_3_), channel_id=1, source_target_pairs={{0,1},{1,0},{2,3},{3,2},{4,5},{5,4},{6,7},{7,6},{8,9},{9,8},{10,11... | collective-permute-start | bytes 786440 | tf_op jit(solution)/shard_map/ppermute | solution.py:173
  18.7 4.0 %collective-permute-start.6 = (bf16[8,64,256]{2,1,0:T(8,128)(2,1)S(1)}, bf16[8,64,256]{2,1,0:T(8,128)(2,1)S(1)}, u32[]{:S(2)}, u32[]{:S(2)}) collective-permute-start(bf16[8,64,256]{2,1,0:T(8,128)(2,1)S(1)} %collective-permute-done.5.refs_5_), channel_id=1, source_target_pairs={{0,1},{1,0},{2,3},{3,2},{4,5},{5,4},{6,7},{7,6},{8,9},{9,8},{10,11... | collective-permute-start | bytes 786440 | tf_op jit(solution)/shard_map/ppermute | solution.py:173
  22.7 3.1 %collective-permute-start.13 = (bf16[8,64,256]{2,1,0:T(8,128)(2,1)S(1)}, bf16[8,64,256]{2,1,0:T(8,128)(2,1)S(1)}, u32[]{:S(2)}, u32[]{:S(2)}) collective-permute-start(bf16[8,64,256]{2,1,0:T(8,128)(2,1)S(1)} %collective-permute-done.12.refs_3_), channel_id=1, source_target_pairs={{7,6},{6,7},{5,4},{4,5},{3,2},{2,3},{1,0},{0,1},{15,14},{14,15},{1... | collective-permute-start | bytes 786440 | tf_op jit(solution)/shard_map/ppermute | solution.py:173
  25.8 4.0 %collective-permute-start.15 = (bf16[8,64,256]{2,1,0:T(8,128)(2,1)S(1)}, bf16[8,64,256]{2,1,0:T(8,128)(2,1)S(1)}, u32[]{:S(2)}, u32[]{:S(2)}) collective-permute-start(bf16[8,64,256]{2,1,0:T(8,128)(2,1)S(1)} %collective-permute-done.14.refs_5_), channel_id=1, source_target_pairs={{7,6},{6,7},{5,4},{4,5},{3,2},{2,3},{1,0},{0,1},{15,14},{14,15},{1... | collective-permute-start | bytes 786440 | tf_op jit(solution)/shard_map/ppermute | solution.py:173
  29.8 1.9 %copy-done = bf16[4,6,256,256]{3,2,1,0:T(8,128)(2,1)S(1)} copy-done((bf16[4,6,256,256]{3,2,1,0:T(8,128)(2,1)S(1)}, bf16[4,6,256,256]{3,2,1,0:T(8,128)(2,1)}, u32[]{:S(2)}) %copy-start) | copy-done | bytes 3145752
  32.0 1.8 %product.2 = (f32[4,64,256]{2,1,0:T(8,128)S(1)}, s16[272,256]{1,0:T(8,128)(2,1)S(1)}, s16[272,256]{1,0:T(8,128)(2,1)S(1)}, s16[272,256]{1,0:T(8,128)(2,1)S(1)}) custom-call(s32[4,6]{1,0:T(4,128)S(1)} %copy-done.2, s32[4]{0:T(128)S(1)} %bitcast.1, bf16[8,64,256]{2,1,0:T(8,128)(2,1)S(1)} %get-tuple-element.19.refs_0_, ...), custom_call_target="tpu_custom_call" | custom-call | flops 805306368 | bytes 3145728 | tf_op jit(solution)/shard_map/product/pallas_call | solution.py:210
  33.8 1.6 %collective-permute-start.7 = (s16[272,256]{1,0:T(8,128)(2,1)S(1)}, s16[272,256]{1,0:T(8,128)(2,1)S(1)}, u32[]{:S(2)}, u32[]{:S(2)}) collective-permute-start(s16[272,256]{1,0:T(8,128)(2,1)S(1)} %get-tuple-element.20), channel_id=1, source_target_pairs={{0,8},{8,0},{16,24},{24,16},{1,9},{9,1},{17,25},{25,17},{2,10},{10... | collective-permute-start | bytes 417800 | tf_op jit(solution)/shard_map/ppermute | solution.py:128
  35.4 1.5 %collective-permute-start.8 = (s16[272,256]{1,0:T(8,128)(2,1)S(1)}, s16[272,256]{1,0:T(8,128)(2,1)S(1)}, u32[]{:S(2)}, u32[]{:S(2)}) collective-permute-start(s16[272,256]{1,0:T(8,128)(2,1)S(1)} %get-tuple-element.21), channel_id=1, source_target_pairs={{0,16},{8,24},{16,0},{24,8},{1,17},{9,25},{17,1},{25,9},{2,18},{10... | collective-permute-start | bytes 417800 | tf_op jit(solution)/shard_map/ppermute | solution.py:128
  37.4 1.8 %product.3 = (f32[4,64,256]{2,1,0:T(8,128)S(1)}, s16[272,256]{1,0:T(8,128)(2,1)S(1)}, s16[272,256]{1,0:T(8,128)(2,1)S(1)}, s16[272,256]{1,0:T(8,128)(2,1)S(1)}) custom-call(s32[4,6]{1,0:T(4,128)S(1)} %copy-done.2, s32[4]{0:T(128)S(1)} %bitcast.2, bf16[8,64,256]{2,1,0:T(8,128)(2,1)S(1)} %get-tuple-element.25.refs_0_, ...), custom_call_target="tpu_custom_call" | custom-call | flops 805306368 | bytes 3145728 | tf_op jit(solution)/shard_map/product/pallas_call | solution.py:210
  39.2 1.6 %collective-permute-start.16 = (s16[272,256]{1,0:T(8,128)(2,1)S(1)}, s16[272,256]{1,0:T(8,128)(2,1)S(1)}, u32[]{:S(2)}, u32[]{:S(2)}) collective-permute-start(s16[272,256]{1,0:T(8,128)(2,1)S(1)} %get-tuple-element.26), channel_id=1, source_target_pairs={{24,16},{16,24},{8,0},{0,8},{25,17},{17,25},{9,1},{1,9},{26,18},{1... | collective-permute-start | bytes 417800 | tf_op jit(solution)/shard_map/ppermute | solution.py:128
  40.8 1.5 %collective-permute-start.17 = (s16[272,256]{1,0:T(8,128)(2,1)S(1)}, s16[272,256]{1,0:T(8,128)(2,1)S(1)}, u32[]{:S(2)}, u32[]{:S(2)}) collective-permute-start(s16[272,256]{1,0:T(8,128)(2,1)S(1)} %get-tuple-element.27), channel_id=1, source_target_pairs={{24,8},{16,0},{8,24},{0,16},{25,9},{17,1},{9,25},{1,17},{26,10},{1... | collective-permute-start | bytes 417800 | tf_op jit(solution)/shard_map/ppermute | solution.py:128
  42.3 0.6 %collective-permute-start.18 = (s16[272,256]{1,0:T(8,128)(2,1)S(1)}, s16[272,256]{1,0:T(8,128)(2,1)S(1)}, u32[]{:S(2)}, u32[]{:S(2)}) collective-permute-start(s16[272,256]{1,0:T(8,128)(2,1)S(1)} %get-tuple-element.28), channel_id=1, source_target_pairs={{24,0},{16,8},{8,16},{0,24},{25,1},{17,9},{9,17},{1,25},{26,2},{18... | collective-permute-start | bytes 417800 | tf_op jit(solution)/shard_map/ppermute | solution.py:128
  42.9 0.7 %collective-permute-done.8.refs_1_ = s16[272,256]{1,0:T(8,128)(2,1)S(1)} collective-permute-done((s16[272,256]{1,0:T(8,128)(2,1)S(1)}, s16[272,256]{1,0:T(8,128)(2,1)S(1)}, u32[]{:S(2)}, u32[]{:S(2)}) %collective-permute-start.8) | collective-permute-done | bytes 139296 | tf_op jit(solution)/shard_map/ppermute | solution.py:128
  43.6 0.8 %collective-permute-done.9.refs_2_ = s16[272,256]{1,0:T(8,128)(2,1)S(1)} collective-permute-done((s16[272,256]{1,0:T(8,128)(2,1)S(1)}, s16[272,256]{1,0:T(8,128)(2,1)S(1)}, u32[]{:S(2)}, u32[]{:S(2)}) %collective-permute-start.9) | collective-permute-done | bytes 139296 | tf_op jit(solution)/shard_map/ppermute | solution.py:128
  44.6 1.8 %collective-permute-done.16.refs_0_ = s16[272,256]{1,0:T(8,128)(2,1)S(1)} collective-permute-done((s16[272,256]{1,0:T(8,128)(2,1)S(1)}, s16[272,256]{1,0:T(8,128)(2,1)S(1)}, u32[]{:S(2)}, u32[]{:S(2)}) %collective-permute-start.16) | collective-permute-done | bytes 139296 | tf_op jit(solution)/shard_map/ppermute | solution.py:128
  46.4 3.2 %collective-permute-done.17.refs_1_ = s16[272,256]{1,0:T(8,128)(2,1)S(1)} collective-permute-done((s16[272,256]{1,0:T(8,128)(2,1)S(1)}, s16[272,256]{1,0:T(8,128)(2,1)S(1)}, u32[]{:S(2)}, u32[]{:S(2)}) %collective-permute-start.17) | collective-permute-done | bytes 139296 | tf_op jit(solution)/shard_map/ppermute | solution.py:128
  49.8 1.3 %collective-permute-start.19 = (f32[4,256]{1,0:T(4,128)S(1)}, f32[4,256]{1,0:T(4,128)S(1)}, u32[]{:S(2)}, u32[]{:S(2)}) collective-permute-start(f32[4,256]{1,0:T(4,128)S(1)} %get-tuple-element.32.refs_2_), channel_id=1, source_target_pairs={{0,8},{8,0},{16,24},{24,16},{1,9},{9,1},{17,25},{25,17},{2,10},{10... | collective-permute-start | bytes 12296 | tf_op jit(solution)/shard_map/ppermute | solution.py:128
  51.2 0.8 %collective-permute-start.20 = (f32[4,256]{1,0:T(4,128)S(1)}, f32[4,256]{1,0:T(4,128)S(1)}, u32[]{:S(2)}, u32[]{:S(2)}) collective-permute-start(f32[4,256]{1,0:T(4,128)S(1)} %get-tuple-element.32.refs_2_), channel_id=1, source_target_pairs={{0,16},{8,24},{16,0},{24,8},{1,17},{9,25},{17,1},{25,9},{2,18},{10... | collective-permute-start | bytes 12296 | tf_op jit(solution)/shard_map/ppermute | solution.py:128
  52.0 1.4 %collective-permute-start.21 = (f32[4,256]{1,0:T(4,128)S(1)}, f32[4,256]{1,0:T(4,128)S(1)}, u32[]{:S(2)}, u32[]{:S(2)}) collective-permute-start(f32[4,256]{1,0:T(4,128)S(1)} %get-tuple-element.32.refs_2_), channel_id=1, source_target_pairs={{0,24},{8,16},{16,8},{24,0},{1,25},{9,17},{17,9},{25,1},{2,26},{10... | collective-permute-start | bytes 12296 | tf_op jit(solution)/shard_map/ppermute | solution.py:128
  53.5 1.3 %collective-permute-done.20.refs_4_ = f32[4,256]{1,0:T(4,128)S(1)} collective-permute-done((f32[4,256]{1,0:T(4,128)S(1)}, f32[4,256]{1,0:T(4,128)S(1)}, u32[]{:S(2)}, u32[]{:S(2)}) %collective-permute-start.20) | collective-permute-done | bytes 4128 | tf_op jit(solution)/shard_map/ppermute | solution.py:128
  54.8 1.7 %collective-permute-done.21.refs_5_ = f32[4,256]{1,0:T(4,128)S(1)} collective-permute-done((f32[4,256]{1,0:T(4,128)S(1)}, f32[4,256]{1,0:T(4,128)S(1)}, u32[]{:S(2)}, u32[]{:S(2)}) %collective-permute-start.21) | collective-permute-done | bytes 4128 | tf_op jit(solution)/shard_map/ppermute | solution.py:128
  56.5 0.7 %scale.1 = bf16[2,4,64,256]{3,2,1,0:T(8,128)(2,1)} custom-call(f32[4,64,256]{2,1,0:T(8,128)S(1)} %get-tuple-element.24.refs_0_, f32[4,64,256]{2,1,0:T(8,128)S(1)} %get-tuple-element.31.refs_1_, f32[4,256]{1,0:T(4,128)S(1)} %get-tuple-element.32.refs_2_, f32[4,256]{1,0:T(4,128)S(1)} %collective-permute-done.19.refs_3_, ...), custom_call_target="tpu_custom_call" | custom-call | tf_op jit(solution)/shard_map/scale/pallas_call | solution.py:229
  (27 shorter events, 2.1 us)
Async XLA Ops:
  0.0 1.9 %collective-permute-start = (bf16[2,8,32,256]{3,2,1,0:T(8,128)(2,1)}, bf16[2,8,32,256]{3,2,1,0:T(8,128)(2,1)S(1)}, u32[]{:S(2)}, u32[]{:S(2)}) collective-permute-start(bf16[2,8,32,256]{3,2,1,0:T(8,128)(2,1)} %mine_ref.1), channel_id=1, source_target_pairs={{0,1},{1,0},{2,3},{3,2},{4,5},{5,4},{6,7},{7,6},{8,9},{9,8},{10,11... | collective-permute-start | bytes 786440 | tf_op jit(solution)/shard_map/ppermute | solution.py:152
  1.9 0.9 %copy-start.1 = (bf16[2,8,32,256]{3,2,1,0:T(8,128)(2,1)S(1)}, bf16[2,8,32,256]{3,2,1,0:T(8,128)(2,1)}, u32[]{:S(2)}) copy-start(bf16[2,8,32,256]{3,2,1,0:T(8,128)(2,1)} %mine_ref.1) | copy-start | bytes 786436
  2.9 29.1 %copy-start.2 = (s32[4,6]{1,0:T(4,128)S(1)}, s32[4,6]{1,0:T(4,128)}, u32[]{:S(2)}) copy-start(s32[4,6]{1,0:T(4,128)} %index_ref.3) | copy-start | bytes 292
  2.9 8.7 %collective-permute-start.1 = (bf16[8,64,256]{2,1,0:T(8,128)(2,1)S(1)}, bf16[8,64,256]{2,1,0:T(8,128)(2,1)S(1)}, u32[]{:S(2)}, u32[]{:S(2)}) collective-permute-start(bf16[8,64,256]{2,1,0:T(8,128)(2,1)S(1)} %get-tuple-element.19.refs_0_), channel_id=1, source_target_pairs={{0,2},{2,4},{4,6},{7,5},{5,3},{3,1},{8,10},{10,12},{12,14},{15,13}... | collective-permute-start | bytes 786440 | tf_op jit(solution)/shard_map/ppermute | solution.py:168
  7.7 24.3 %copy-start.3 = (s32[4,1]{0,1:T(1,128)S(1)}, s32[4,1]{0,1:T(1,128)}, u32[]{:S(2)}) copy-start(s32[4,1]{0,1:T(1,128)} %param.7) | copy-start | bytes 52
  7.7 7.3 %collective-permute-start.10 = (bf16[8,64,256]{2,1,0:T(8,128)(2,1)S(1)}, bf16[8,64,256]{2,1,0:T(8,128)(2,1)S(1)}, u32[]{:S(2)}, u32[]{:S(2)}) collective-permute-start(bf16[8,64,256]{2,1,0:T(8,128)(2,1)S(1)} %get-tuple-element.25.refs_0_), channel_id=1, source_target_pairs={{3,1},{5,3},{7,5},{4,6},{2,4},{0,2},{11,9},{13,11},{15,13},{12,14}... | collective-permute-start | bytes 786440 | tf_op jit(solution)/shard_map/ppermute | solution.py:168
  11.6 4.9 %collective-permute-start.3 = (bf16[8,64,256]{2,1,0:T(8,128)(2,1)S(1)}, bf16[8,64,256]{2,1,0:T(8,128)(2,1)S(1)}, u32[]{:S(2)}, u32[]{:S(2)}) collective-permute-start(bf16[8,64,256]{2,1,0:T(8,128)(2,1)S(1)} %collective-permute-done.1.refs_1_), channel_id=1, source_target_pairs={{2,4},{4,6},{5,3},{3,1},{10,12},{12,14},{13,11},{11,9},{18,20},{20... | collective-permute-start | bytes 786440 | tf_op jit(solution)/shard_map/ppermute | solution.py:169
  12.3 6.5 %collective-permute-start.5 = (bf16[8,64,256]{2,1,0:T(8,128)(2,1)S(1)}, bf16[8,64,256]{2,1,0:T(8,128)(2,1)S(1)}, u32[]{:S(2)}, u32[]{:S(2)}) collective-permute-start(bf16[8,64,256]{2,1,0:T(8,128)(2,1)S(1)} %collective-permute-done.1.refs_1_), channel_id=1, source_target_pairs={{2,6},{5,1},{10,14},{13,9},{18,22},{21,17},{26,30},{29,25}} | collective-permute-start | bytes 786440 | tf_op jit(solution)/shard_map/ppermute | solution.py:170
  13.0 9.8 %collective-permute-start.2 = (bf16[8,64,256]{2,1,0:T(8,128)(2,1)S(1)}, bf16[8,64,256]{2,1,0:T(8,128)(2,1)S(1)}, u32[]{:S(2)}, u32[]{:S(2)}) collective-permute-start(bf16[8,64,256]{2,1,0:T(8,128)(2,1)S(1)} %collective-permute-done.1.refs_1_), channel_id=1, source_target_pairs={{0,1},{1,0},{2,3},{3,2},{4,5},{5,4},{6,7},{7,6},{8,9},{9,8},{10,11... | collective-permute-start | bytes 786440 | tf_op jit(solution)/shard_map/ppermute | solution.py:173
  15.1 7.6 %collective-permute-start.12 = (bf16[8,64,256]{2,1,0:T(8,128)(2,1)S(1)}, bf16[8,64,256]{2,1,0:T(8,128)(2,1)S(1)}, u32[]{:S(2)}, u32[]{:S(2)}) collective-permute-start(bf16[8,64,256]{2,1,0:T(8,128)(2,1)S(1)} %collective-permute-done.10.refs_1_), channel_id=1, source_target_pairs={{3,1},{5,3},{4,6},{2,4},{11,9},{13,11},{12,14},{10,12},{19,17},{21... | collective-permute-start | bytes 786440 | tf_op jit(solution)/shard_map/ppermute | solution.py:169
  15.8 10.1 %collective-permute-start.14 = (bf16[8,64,256]{2,1,0:T(8,128)(2,1)S(1)}, bf16[8,64,256]{2,1,0:T(8,128)(2,1)S(1)}, u32[]{:S(2)}, u32[]{:S(2)}) collective-permute-start(bf16[8,64,256]{2,1,0:T(8,128)(2,1)S(1)} %collective-permute-done.10.refs_1_), channel_id=1, source_target_pairs={{5,1},{2,6},{13,9},{10,14},{21,17},{18,22},{29,25},{26,30}} | collective-permute-start | bytes 786440 | tf_op jit(solution)/shard_map/ppermute | solution.py:170
  16.5 15.5 %collective-permute-start.4 = (bf16[8,64,256]{2,1,0:T(8,128)(2,1)S(1)}, bf16[8,64,256]{2,1,0:T(8,128)(2,1)S(1)}, u32[]{:S(2)}, u32[]{:S(2)}) collective-permute-start(bf16[8,64,256]{2,1,0:T(8,128)(2,1)S(1)} %collective-permute-done.3.refs_3_), channel_id=1, source_target_pairs={{0,1},{1,0},{2,3},{3,2},{4,5},{5,4},{6,7},{7,6},{8,9},{9,8},{10,11... | collective-permute-start | bytes 786440 | tf_op jit(solution)/shard_map/ppermute | solution.py:173
  18.7 13.2 %collective-permute-start.6 = (bf16[8,64,256]{2,1,0:T(8,128)(2,1)S(1)}, bf16[8,64,256]{2,1,0:T(8,128)(2,1)S(1)}, u32[]{:S(2)}, u32[]{:S(2)}) collective-permute-start(bf16[8,64,256]{2,1,0:T(8,128)(2,1)S(1)} %collective-permute-done.5.refs_5_), channel_id=1, source_target_pairs={{0,1},{1,0},{2,3},{3,2},{4,5},{5,4},{6,7},{7,6},{8,9},{9,8},{10,11... | collective-permute-start | bytes 786440 | tf_op jit(solution)/shard_map/ppermute | solution.py:173
  22.7 14.2 %collective-permute-start.11 = (bf16[8,64,256]{2,1,0:T(8,128)(2,1)S(1)}, bf16[8,64,256]{2,1,0:T(8,128)(2,1)S(1)}, u32[]{:S(2)}, u32[]{:S(2)}) collective-permute-start(bf16[8,64,256]{2,1,0:T(8,128)(2,1)S(1)} %collective-permute-done.10.refs_1_), channel_id=1, source_target_pairs={{7,6},{6,7},{5,4},{4,5},{3,2},{2,3},{1,0},{0,1},{15,14},{14,15},{1... | collective-permute-start | bytes 786440 | tf_op jit(solution)/shard_map/ppermute | solution.py:173
  22.7 14.7 %collective-permute-start.13 = (bf16[8,64,256]{2,1,0:T(8,128)(2,1)S(1)}, bf16[8,64,256]{2,1,0:T(8,128)(2,1)S(1)}, u32[]{:S(2)}, u32[]{:S(2)}) collective-permute-start(bf16[8,64,256]{2,1,0:T(8,128)(2,1)S(1)} %collective-permute-done.12.refs_3_), channel_id=1, source_target_pairs={{7,6},{6,7},{5,4},{4,5},{3,2},{2,3},{1,0},{0,1},{15,14},{14,15},{1... | collective-permute-start | bytes 786440 | tf_op jit(solution)/shard_map/ppermute | solution.py:173
  25.8 11.6 %collective-permute-start.15 = (bf16[8,64,256]{2,1,0:T(8,128)(2,1)S(1)}, bf16[8,64,256]{2,1,0:T(8,128)(2,1)S(1)}, u32[]{:S(2)}, u32[]{:S(2)}) collective-permute-start(bf16[8,64,256]{2,1,0:T(8,128)(2,1)S(1)} %collective-permute-done.14.refs_5_), channel_id=1, source_target_pairs={{7,6},{6,7},{5,4},{4,5},{3,2},{2,3},{1,0},{0,1},{15,14},{14,15},{1... | collective-permute-start | bytes 786440 | tf_op jit(solution)/shard_map/ppermute | solution.py:173
  29.8 1.9 %copy-start = (bf16[4,6,256,256]{3,2,1,0:T(8,128)(2,1)S(1)}, bf16[4,6,256,256]{3,2,1,0:T(8,128)(2,1)}, u32[]{:S(2)}) copy-start(bf16[4,6,256,256]{3,2,1,0:T(8,128)(2,1)} %right_ref.1) | copy-start | bytes 9437188
  33.8 8.5 %collective-permute-start.7 = (s16[272,256]{1,0:T(8,128)(2,1)S(1)}, s16[272,256]{1,0:T(8,128)(2,1)S(1)}, u32[]{:S(2)}, u32[]{:S(2)}) collective-permute-start(s16[272,256]{1,0:T(8,128)(2,1)S(1)} %get-tuple-element.20), channel_id=1, source_target_pairs={{0,8},{8,0},{16,24},{24,16},{1,9},{9,1},{17,25},{25,17},{2,10},{10... | collective-permute-start | bytes 417800 | tf_op jit(solution)/shard_map/ppermute | solution.py:128
  35.4 8.2 %collective-permute-start.8 = (s16[272,256]{1,0:T(8,128)(2,1)S(1)}, s16[272,256]{1,0:T(8,128)(2,1)S(1)}, u32[]{:S(2)}, u32[]{:S(2)}) collective-permute-start(s16[272,256]{1,0:T(8,128)(2,1)S(1)} %get-tuple-element.21), channel_id=1, source_target_pairs={{0,16},{8,24},{16,0},{24,8},{1,17},{9,25},{17,1},{25,9},{2,18},{10... | collective-permute-start | bytes 417800 | tf_op jit(solution)/shard_map/ppermute | solution.py:128
  36.9 7.5 %collective-permute-start.9 = (s16[272,256]{1,0:T(8,128)(2,1)S(1)}, s16[272,256]{1,0:T(8,128)(2,1)S(1)}, u32[]{:S(2)}, u32[]{:S(2)}) collective-permute-start(s16[272,256]{1,0:T(8,128)(2,1)S(1)} %get-tuple-element.22), channel_id=1, source_target_pairs={{0,24},{8,16},{16,8},{24,0},{1,25},{9,17},{17,9},{25,1},{2,26},{10... | collective-permute-start | bytes 417800 | tf_op jit(solution)/shard_map/ppermute | solution.py:128
  39.2 7.2 %collective-permute-start.16 = (s16[272,256]{1,0:T(8,128)(2,1)S(1)}, s16[272,256]{1,0:T(8,128)(2,1)S(1)}, u32[]{:S(2)}, u32[]{:S(2)}) collective-permute-start(s16[272,256]{1,0:T(8,128)(2,1)S(1)} %get-tuple-element.26), channel_id=1, source_target_pairs={{24,16},{16,24},{8,0},{0,8},{25,17},{17,25},{9,1},{1,9},{26,18},{1... | collective-permute-start | bytes 417800 | tf_op jit(solution)/shard_map/ppermute | solution.py:128
  40.8 8.9 %collective-permute-start.17 = (s16[272,256]{1,0:T(8,128)(2,1)S(1)}, s16[272,256]{1,0:T(8,128)(2,1)S(1)}, u32[]{:S(2)}, u32[]{:S(2)}) collective-permute-start(s16[272,256]{1,0:T(8,128)(2,1)S(1)} %get-tuple-element.27), channel_id=1, source_target_pairs={{24,8},{16,0},{8,24},{0,16},{25,9},{17,1},{9,25},{1,17},{26,10},{1... | collective-permute-start | bytes 417800 | tf_op jit(solution)/shard_map/ppermute | solution.py:128
  42.3 7.3 %collective-permute-start.18 = (s16[272,256]{1,0:T(8,128)(2,1)S(1)}, s16[272,256]{1,0:T(8,128)(2,1)S(1)}, u32[]{:S(2)}, u32[]{:S(2)}) collective-permute-start(s16[272,256]{1,0:T(8,128)(2,1)S(1)} %get-tuple-element.28), channel_id=1, source_target_pairs={{24,0},{16,8},{8,16},{0,24},{25,1},{17,9},{9,17},{1,25},{26,2},{18... | collective-permute-start | bytes 417800 | tf_op jit(solution)/shard_map/ppermute | solution.py:128
  49.8 3.7 %collective-permute-start.19 = (f32[4,256]{1,0:T(4,128)S(1)}, f32[4,256]{1,0:T(4,128)S(1)}, u32[]{:S(2)}, u32[]{:S(2)}) collective-permute-start(f32[4,256]{1,0:T(4,128)S(1)} %get-tuple-element.32.refs_2_), channel_id=1, source_target_pairs={{0,8},{8,0},{16,24},{24,16},{1,9},{9,1},{17,25},{25,17},{2,10},{10... | collective-permute-start | bytes 12296 | tf_op jit(solution)/shard_map/ppermute | solution.py:128
  51.2 3.6 %collective-permute-start.20 = (f32[4,256]{1,0:T(4,128)S(1)}, f32[4,256]{1,0:T(4,128)S(1)}, u32[]{:S(2)}, u32[]{:S(2)}) collective-permute-start(f32[4,256]{1,0:T(4,128)S(1)} %get-tuple-element.32.refs_2_), channel_id=1, source_target_pairs={{0,16},{8,24},{16,0},{24,8},{1,17},{9,25},{17,1},{25,9},{2,18},{10... | collective-permute-start | bytes 12296 | tf_op jit(solution)/shard_map/ppermute | solution.py:128
  52.0 4.5 %collective-permute-start.21 = (f32[4,256]{1,0:T(4,128)S(1)}, f32[4,256]{1,0:T(4,128)S(1)}, u32[]{:S(2)}, u32[]{:S(2)}) collective-permute-start(f32[4,256]{1,0:T(4,128)S(1)} %get-tuple-element.32.refs_2_), channel_id=1, source_target_pairs={{0,24},{8,16},{16,8},{24,0},{1,25},{9,17},{17,9},{25,1},{2,26},{10... | collective-permute-start | bytes 12296 | tf_op jit(solution)/shard_map/ppermute | solution.py:128
